TPU v7x, 256 devices: a whole 4x4x8 slice. The times are simulated.
256 devices in a mesh: dp: 8 (over y_lo, x), ctx: 32 (over y_hi, z, core).
Axes of the slice: x: 4, y: 4 (y_hi: 2, y_lo: 2; y = y_hi * 2 + y_lo), z: 8, core: 2. Of those that a mesh axis runs over, the one named last changes fastest.
Arguments:
- query_rows: bfloat16 [32768, 2048], P(('dp', 'ctx')), may hold values from -64 to 64
- key_rows: bfloat16 [32768, 2048], P(('dp', 'ctx')), may hold values from -64 to 64
- value_rows: bfloat16 [32768, 2048], P(('dp', 'ctx')), may hold values from -6 to 6
- cotangent: bfloat16 [32768, 2048], P(('dp', 'ctx')), may hold values from -6 to 6
- query_gain: float32 [2048], replicated, may hold values from 0.5 to 5.5
- key_gain: float32 [2048], replicated, may hold values from 0.5 to 5.5
- positions: int32 [32768], P(('dp', 'ctx')), may hold values from 0 to 2047, as said below
- span_start: int32 [16, 2], P('dp'), may hold values from 0 to 1536, as said below
- span_length: int32 [16, 2], P('dp'), may hold values from 256 to 512
Outputs:
- output: bfloat16 [32768, 2048], P(('dp', 'ctx'))
- query_grad: bfloat16 [32768, 2048], P(('dp', 'ctx'))
- key_grad: bfloat16 [32768, 2048], P(('dp', 'ctx'))
- value_grad: bfloat16 [32768, 2048], P(('dp', 'ctx'))
- gain_grads: float32 [2, 2048], replicated
Inputs may be any that keep to these rules, and one draw needn't show every extreme that they name: Within each sequence every position 0 to 2047 appears once; each block's rows are two runs of 64 consecutive positions, each run in increasing order. `span_start`: the first span of a sequence starts at 512 or earlier, the second at 1024 or later; spans don't intersect and end inside the sequence.
All inputs are finite; a program needn't handle non-finite values.
Results may differ from a plain program's by a relative error of at most 0.035.
The roundings to bfloat16 on the way count: a program that leaves them out, or rounds other values in their place, can miss the bound.
Values may be sent and summed in bfloat16 or wider, within the bound.
A program may use at most 128 MiB of HBM per device.

v0:
```python
import jax
import jax.numpy as jnp
from jax import lax
from jax.sharding import Mesh
from jax.sharding import PartitionSpec as P

HEADS = 16
HEAD = 128
SEQS_CTX = 2
CTX = ("ctx_0", "ctx_1", "ctx_2")
DP_CTX = ("dp_0", "dp_1", "ctx_0", "ctx_1", "ctx_2")
DP = ("dp_0", "dp_1")


epsilon = 1e-05
masked_score = -1e30


def in_one_piece(arrays, axis, split_dim, concat_dim, along):
    ends, at = ([], 0)
    for a in arrays[:-1]:
        at += a.shape[along]
        ends.append(at)
    both = jnp.concatenate(arrays, axis=along)
    return tuple(
        jnp.split(
            lax.all_to_all(both, axis, split_axis=split_dim, concat_axis=concat_dim, tiled=True),
            ends,
            axis=along,
        )
    )


def laid_out(blocks, dim):
    blocks = jnp.moveaxis(blocks, 0, dim)
    lengths = blocks.shape
    return blocks.reshape(*lengths[:dim], lengths[dim] * lengths[dim + 1], *lengths[dim + 2 :])


def sent_to_all(shard, axis):
    peers = lax.axis_size(axis)
    return lax.all_to_all(
        jnp.broadcast_to(shard[None], (peers, *shard.shape)), axis, 0, 0, tiled=True
    )


def gather_directly(shard, axis, dim):
    return laid_out(sent_to_all(shard, axis), dim)


def one_axis_at_a_time(shard, axes):
    for axis in axes:
        shard = lax.psum(shard, axis)
    return shard


def normalize(raw_rows, gain_row):
    values = raw_rows.astype(jnp.float32).reshape(raw_rows.shape[0], HEADS, HEAD)
    inverse = lax.rsqrt(jnp.mean(values * values, axis=-1, keepdims=True) + epsilon)
    unit_rows = values * inverse
    return (unit_rows, inverse, (unit_rows * gain_row.reshape(HEADS, HEAD)).astype(jnp.bfloat16))


def norm_backward(grad_normed, unit_rows, inverse, gain_row):
    grad_unit = grad_normed * gain_row.reshape(HEADS, HEAD)
    projected = jnp.mean(grad_unit * unit_rows, axis=-1, keepdims=True)
    grad_raw = inverse * (grad_unit - unit_rows * projected)
    gain_part = jnp.sum(grad_normed * unit_rows, axis=0).reshape(HEADS * HEAD)
    return (grad_raw.reshape(grad_raw.shape[0], HEADS * HEAD).astype(jnp.bfloat16), gain_part)


def span_labels(places, starts, lengths):
    inside = (places[:, None] >= starts[None, :]) & (
        places[:, None] < starts[None, :] + lengths[None, :]
    )
    span_ids = jnp.arange(1, starts.shape[0] + 1, dtype=jnp.int32)
    return jnp.sum(jnp.where(inside, span_ids[None, :], 0), axis=1)


def visible(query_places, query_labels, key_places, key_labels):
    causal = key_places[None, :] <= query_places[:, None]
    same_span = (query_labels[:, None] == key_labels[None, :]) & (query_labels[:, None] > 0)
    return causal | same_span


def block_scores(query_block, key_block, allowed):
    score_scale = HEAD ** (-0.5)
    scores = (
        jnp.einsum("qhd,khd->hqk", query_block, key_block, preferred_element_type=jnp.float32)
        * score_scale
    )
    return jnp.where(allowed[None], scores, masked_score)


def full_attention(packed):
    query_pack, key_pack, query_places, key_places, starts, lengths = packed
    query_block, grads_block = (query_pack[0], query_pack[1])
    key_block, value_block = (key_pack[0], key_pack[1])
    score_scale = HEAD ** (-0.5)
    allowed = visible(
        query_places,
        span_labels(query_places, starts, lengths),
        key_places,
        span_labels(key_places, starts, lengths),
    )
    scores = block_scores(query_block, key_block, allowed)
    row_max = jnp.max(scores, axis=-1, keepdims=True)
    log_total = row_max + jnp.log(jnp.sum(jnp.exp(scores - row_max), axis=-1, keepdims=True))
    attn_probs = jnp.exp(scores - log_total)
    weights = attn_probs.astype(jnp.bfloat16)
    output = jnp.einsum(
        "hqk,khd->qhd", weights, value_block, preferred_element_type=jnp.float32
    ).astype(jnp.bfloat16)
    row_delta = jnp.einsum("qhd,qhd->hq", output, grads_block, preferred_element_type=jnp.float32)
    grad_values = jnp.einsum(
        "hqk,qhd->khd", weights, grads_block, preferred_element_type=jnp.float32
    )
    prob_grads = jnp.einsum(
        "qhd,khd->hqk", grads_block, value_block, preferred_element_type=jnp.float32
    )
    score_grads = (attn_probs * (prob_grads - row_delta[..., None])).astype(jnp.bfloat16)
    grad_query = (
        jnp.einsum("hqk,khd->qhd", score_grads, key_block, preferred_element_type=jnp.float32)
        * score_scale
    )
    grad_keys = (
        jnp.einsum("hqk,qhd->khd", score_grads, query_block, preferred_element_type=jnp.float32)
        * score_scale
    )
    return (output.astype(jnp.float32), grad_query, jnp.stack([grad_keys, grad_values]))


def by_head_groups(
    query_normed,
    key_normed,
    value_heads,
    out_grads,
    all_places,
    span_start,
    span_length,
    ctx_index,
    axis_count,
):
    row_count = query_normed.shape[0]
    members = axis_count // SEQS_CTX
    row_parts = max(1, axis_count // HEADS)
    per_device = max(1, HEADS // axis_count)
    groups = HEADS // per_device
    piece_rows = row_count // row_parts
    query_piece = ctx_index % row_parts

    def by_heads(tensor):
        return jnp.transpose(tensor.reshape(row_count, groups, per_device, HEAD), (1, 0, 2, 3))

    def by_pieces(tensor):
        shaped = tensor.reshape(row_parts, piece_rows, groups, per_device, HEAD)
        return jnp.transpose(shaped, (2, 0, 1, 3, 4)).reshape(
            axis_count, piece_rows, per_device, HEAD
        )

    key_send = jnp.repeat(
        jnp.stack([by_heads(key_normed), by_heads(value_heads)], axis=1), row_parts, axis=0
    )
    query_send = jnp.stack([by_pieces(query_normed), by_pieces(out_grads)], axis=1)
    key_in, query_in = in_one_piece((key_send, query_send), CTX, 0, 0, 2)

    def sequence_major(tensor):
        shaped = tensor.reshape((members, SEQS_CTX) + tensor.shape[1:])
        return jnp.swapaxes(shaped, 0, 1)

    key_pack = jnp.swapaxes(sequence_major(key_in), 1, 2).reshape(
        SEQS_CTX, 2, members * row_count, per_device, HEAD
    )
    query_pack = jnp.swapaxes(sequence_major(query_in), 1, 2).reshape(
        SEQS_CTX, 2, members * piece_rows, per_device, HEAD
    )
    place_table = sequence_major(all_places.reshape(axis_count, row_count))
    key_places = place_table.reshape(SEQS_CTX, members * row_count)
    query_places = lax.dynamic_index_in_dim(
        place_table.reshape(SEQS_CTX, members, row_parts, piece_rows),
        query_piece,
        2,
        keepdims=False,
    )
    query_places = query_places.reshape(SEQS_CTX, members * piece_rows)
    out_seq, query_seq, kv_seq = lax.map(
        full_attention, (query_pack, key_pack, query_places, key_places, span_start, span_length)
    )

    def source_major(tensor, rows):
        shaped = tensor.reshape((SEQS_CTX, members, rows) + tensor.shape[2:])
        return jnp.swapaxes(shaped, 0, 1).reshape((axis_count, rows) + tensor.shape[2:])

    rows_send = jnp.stack(
        [source_major(out_seq, piece_rows), source_major(query_seq, piece_rows)], axis=1
    )
    kv_send = source_major(jnp.swapaxes(kv_seq, 1, 2), row_count)
    rows_back, keys_back = (
        lax.all_to_all(
            rows_send.astype(jnp.bfloat16), CTX, split_axis=0, concat_axis=0, tiled=True
        ).astype(rows_send.dtype),
        lax.all_to_all(
            kv_send.astype(jnp.bfloat16), CTX, split_axis=0, concat_axis=0, tiled=True
        ).astype(kv_send.dtype),
    )
    rows_back = jnp.transpose(
        rows_back.reshape(groups, row_parts, 2, piece_rows, per_device, HEAD), (2, 1, 3, 0, 4, 5)
    ).reshape(2, row_count, HEADS, HEAD)
    keys_back = jnp.sum(
        keys_back.reshape(groups, row_parts, row_count, 2, per_device, HEAD), axis=1
    )
    keys_back = jnp.transpose(keys_back, (2, 1, 0, 3, 4)).reshape(2, row_count, HEADS, HEAD)
    return (rows_back[0].astype(jnp.bfloat16), rows_back[1], keys_back[0], keys_back[1])


def body(
    query_rows,
    key_rows,
    value_rows,
    cotangent,
    query_gain,
    key_gain,
    positions,
    span_start,
    span_length,
):
    row_count = query_rows.shape[0]
    axis_count = lax.axis_size(CTX)
    ctx_index = lax.axis_index(CTX)
    query_unit, query_inverse, query_normed = normalize(query_rows, query_gain)
    key_unit, key_inverse, key_normed = normalize(key_rows, key_gain)
    value_heads = value_rows.reshape(row_count, HEADS, HEAD)
    out_grads = cotangent.reshape(row_count, HEADS, HEAD)
    all_places = gather_directly(positions, CTX, 0)
    output, grad_query, grad_keys, grad_values = by_head_groups(
        query_normed,
        key_normed,
        value_heads,
        out_grads,
        all_places,
        span_start,
        span_length,
        ctx_index,
        axis_count,
    )
    query_grad, query_part = norm_backward(grad_query, query_unit, query_inverse, query_gain)
    key_grad, key_part = norm_backward(grad_keys, key_unit, key_inverse, key_gain)
    gain_grads = one_axis_at_a_time(jnp.stack([query_part, key_part]), DP_CTX)
    value_grad = grad_values.reshape(row_count, HEADS * HEAD).astype(jnp.bfloat16)
    return (output.reshape(row_count, HEADS * HEAD), query_grad, key_grad, value_grad, gain_grads)


def solution(mesh):
    split = Mesh(mesh.devices.reshape(2, 4, 2, 8, 2), ("dp_0", "dp_1", "ctx_0", "ctx_1", "ctx_2"))
    placed = (
        P(DP_CTX, None),
        P(DP_CTX, None),
        P(DP_CTX, None),
        P(DP_CTX, None),
        P(),
        P(),
        P(DP_CTX),
        P(DP, None),
        P(DP, None),
    )
    return jax.shard_map(
        body,
        mesh=split,
        in_specs=placed,
        out_specs=(P(DP_CTX, None), P(DP_CTX, None), P(DP_CTX, None), P(DP_CTX, None), P()),
        check_vma=False,
    )
```

profile of v0, /device:TPU:32, one launch (start us, length us, event | category | flops | bytes accessed | tf_op | source)
XLA Modules:
  0.0 343.9 jit_solution(11219863385474828585)
XLA Ops:
  0.6 1.3 broadcast_in_dim.84
  2.0 11.4 %all-to-all-start.1 = ((s32[32,1,128]{2,1,0:T(1,128)}), s32[32,1,128]{2,1,0:T(1,128)S(1)}, u32[]{:S(2)}, u32[]{:S(2)}) async-start(s32[32,1,128]{2,1,0:T(1,128)} %broadcast_in_dim.84), calls=%async_computation.1 | async-start | bytes 32768 | tf_op jit(solution)/shard_map/all_to_all | solution.py:42
  13.3 1.1 fusion.14
  14.5 1.1 convert_bitcast_fusion
  15.6 1.3 copy.176
  18.0 1.1 copy.231
  19.3 1.2 copy.230
  20.5 1.6 reduce_sum.93
  25.2 1.1 maximum_bitcast_fusion.1
  27.5 1.8 pad_maximum_fusion
  29.3 9.8 %all-to-all-start = ((bf16[32,2,192,1,128]{4,2,1,3,0:T(8,128)(2,1)}), bf16[32,2,192,1,128]{4,2,1,3,0:T(8,128)(2,1)S(1)}, u32[]{:S(2)}, u32[]{:S(2)}) async-start(bf16[32,2,192,1,128]{4,2,1,3,0:T(8,128)(2,1)} %pad_maximum_fusion), calls=%async_computation | async-start | bytes 6291456 | tf_op jit(solution)/shard_map/all_to_all | solution.py:27
  39.4 73.1 %all-to-all-done = bf16[32,2,192,1,128]{4,2,1,3,0:T(8,128)(2,1)S(1)} async-done(((bf16[32,2,192,1,128]{4,2,1,3,0:T(8,128)(2,1)}), bf16[32,2,192,1,128]{4,2,1,3,0:T(8,128)(2,1)S(1)}, u32[]{:S(2)}, u32[]{:S(2)}) %all-to-all-start) | async-done | bytes 3145760 | tf_op jit(solution)/shard_map/all_to_all | solution.py:27
  112.8 1.5 copy.185
  115.3 61.9 %while.14 = (s32[]{:T(128)}, bf16[2,1024,1,128]{3,1,0,2:T(8,128)(2,1)}, bf16[2,1024,1,128]{3,1,0,2:T(8,128)(2,1)}, bf16[2,2,2048,1,128]{4,2,1,0,3:T(8,128)(2,1)}...) while((s32[]{:T(128)}, ...), condition=%wide.region_7.8_spmd, body=%wide.region_2.7_spmd.sunk | while | flops 3254675456 | bytes 124642640 | solution.py:186
  115.6 4.2 %fusion.51 = (f32[1024]{0:T(1024)S(1)}, f32[1024,2048]{1,0:T(8,128)S(1)}) fusion(bf16[2,2,2048,1,128]{4,2,3,1,0:T(8,128)(2,1)} %get-tuple-element.295, s32[]{:T(128)S(6)} %copy.264, bf16[2,2,1024,1,128]{4,2,3,1,0:T(8,128)(2,1)} %get-tuple-element.300, pred[1024]{0:T(1024)(128)(4,1)S(1)} %broadcast_compare_fusion.2, s32[2048]{0:T(1024)S(1)} %fusion.50, ...), kind=kOutput, calls=%fused_computation.84.clone.1 | convolution fusion | flops 551549952 | bytes 9205760 | tf_op jit(solution)/shard_map/while/body/eval_jaxpr/qhd,khd->hqk/dot_general | solution.py:89
  119.8 1.3 exponential_reduce_fusion.2
  121.1 1.9 copy-done
  123.0 1.5 fusion.52
  124.5 1.7 convolution_bitcast_fusion.2
  126.3 2.6 bitcast_convert_fusion.3
  129.0 1.2 multiply_reduce_fusion.5
  130.2 7.3 %multiply_convert_fusion.4 = bf16[1024,2048]{1,0:T(8,128)(2,1)} fusion(f32[1024,2048]{1,0:T(8,128)} %copy-done, f32[1024]{0:T(1024)S(1)} %multiply_reduce_fusion.5, f32[1024]{0:T(1024)S(1)} %log_add_fusion.2, bf16[2,2,2048,1,128]{4,2,3,1,0:T(8,128)(2,1)} %get-tuple-element.295, s32[]{:T(128)S(6)} %copy.264, s32[]{:T(128)S(6)} %add.93, ...), kind=kOutput, calls=%fused_computation.clone.1 | convolution fusion | flops 545259520 | bytes 13379584 | tf_op jit(solution)/shard_map/while/body/eval_jaxpr/qhd,khd->hqk/dot_general | solution.py:118
  137.7 4.0 %fusion.53 = bf16[1,1024,1,128]{1,3,2,0:T(8,128)(2,1)S(1)} fusion(bf16[1024,2048]{1,0:T(8,128)(2,1)} %multiply_convert_fusion.4, bf16[2,2,2048,1,128]{4,2,3,1,0:T(8,128)(2,1)} %get-tuple-element.295, s32[]{:T(128)S(6)} %copy.264), kind=kOutput, calls=%fused_computation.10.clone.1 | convolution fusion | flops 537133056 | bytes 4980740 | tf_op jit(solution)/shard_map/while/body/eval_jaxpr/hqk,khd->qhd/dot_general | solution.py:123
  141.8 1.7 fusion.54
  146.5 4.2 %fusion.51 = (f32[1024]{0:T(1024)S(1)}, f32[1024,2048]{1,0:T(8,128)S(1)}) fusion(bf16[2,2,2048,1,128]{4,2,3,1,0:T(8,128)(2,1)} %get-tuple-element.295, s32[]{:T(128)S(6)} %copy.264, bf16[2,2,1024,1,128]{4,2,3,1,0:T(8,128)(2,1)} %get-tuple-element.300, pred[1024]{0:T(1024)(128)(4,1)S(1)} %broadcast_compare_fusion.2, s32[2048]{0:T(1024)S(1)} %fusion.50, ...), kind=kOutput, calls=%fused_computation.84.clone.1 | convolution fusion | flops 551549952 | bytes 9205760 | tf_op jit(solution)/shard_map/while/body/eval_jaxpr/qhd,khd->hqk/dot_general | solution.py:89
  150.8 1.3 exponential_reduce_fusion.2
  152.0 1.9 copy-done
  154.0 1.5 fusion.52
  155.5 1.7 convolution_bitcast_fusion.2
  157.2 2.6 bitcast_convert_fusion.3
  160.0 1.2 multiply_reduce_fusion.5
  161.2 7.3 %multiply_convert_fusion.4 = bf16[1024,2048]{1,0:T(8,128)(2,1)} fusion(f32[1024,2048]{1,0:T(8,128)} %copy-done, f32[1024]{0:T(1024)S(1)} %multiply_reduce_fusion.5, f32[1024]{0:T(1024)S(1)} %log_add_fusion.2, bf16[2,2,2048,1,128]{4,2,3,1,0:T(8,128)(2,1)} %get-tuple-element.295, s32[]{:T(128)S(6)} %copy.264, s32[]{:T(128)S(6)} %add.93, ...), kind=kOutput, calls=%fused_computation.clone.1 | convolution fusion | flops 545259520 | bytes 13379584 | tf_op jit(solution)/shard_map/while/body/eval_jaxpr/qhd,khd->hqk/dot_general | solution.py:118
  168.7 4.0 %fusion.53 = bf16[1,1024,1,128]{1,3,2,0:T(8,128)(2,1)S(1)} fusion(bf16[1024,2048]{1,0:T(8,128)(2,1)} %multiply_convert_fusion.4, bf16[2,2,2048,1,128]{4,2,3,1,0:T(8,128)(2,1)} %get-tuple-element.295, s32[]{:T(128)S(6)} %copy.264), kind=kOutput, calls=%fused_computation.10.clone.1 | convolution fusion | flops 537133056 | bytes 4980740 | tf_op jit(solution)/shard_map/while/body/eval_jaxpr/hqk,khd->qhd/dot_general | solution.py:123
  172.7 1.7 fusion.54
  178.3 1.1 copy.194
  180.6 6.5 %all-to-all-start.2 = ((bf16[32,2,64,1,128]{4,2,3,1,0:T(8,128)(2,1)}), bf16[32,2,64,1,128]{4,2,3,1,0:T(8,128)(2,1)S(1)}, u32[]{:S(2)}, u32[]{:S(2)}) async-start(bf16[32,2,64,1,128]{4,2,3,1,0:T(8,128)(2,1)} %copy.195), calls=%async_computation.2 | async-start | bytes 2097152 | tf_op jit(solution)/shard_map/all_to_all | solution.py:199
  187.2 3.3 copy.203
  190.4 27.2 %all-to-all-done.2 = bf16[32,2,64,1,128]{4,2,3,1,0:T(8,128)(2,1)S(1)} async-done(((bf16[32,2,64,1,128]{4,2,3,1,0:T(8,128)(2,1)}), bf16[32,2,64,1,128]{4,2,3,1,0:T(8,128)(2,1)S(1)}, u32[]{:S(2)}, u32[]{:S(2)}) %all-to-all-start.2) | async-done | bytes 1048608 | tf_op jit(solution)/shard_map/all_to_all | solution.py:199
  217.6 4.5 %all-to-all-start.3 = ((bf16[32,128,2,1,128]{4,1,3,2,0:T(8,128)(2,1)}), bf16[32,128,2,1,128]{4,1,3,2,0:T(8,128)(2,1)}, u32[]{:S(2)}, u32[]{:S(2)}) async-start(bf16[32,128,2,1,128]{4,1,3,2,0:T(8,128)(2,1)} %bitcast.251), calls=%async_computation.3 | async-start | bytes 4194304 | tf_op jit(solution)/shard_map/all_to_all | solution.py:202
  222.3 1.3 copy.205
  227.3 1.9 fusion.18
  229.2 45.7 %all-to-all-done.3 = bf16[32,128,2,1,128]{4,1,3,2,0:T(8,128)(2,1)} async-done(((bf16[32,128,2,1,128]{4,1,3,2,0:T(8,128)(2,1)}), bf16[32,128,2,1,128]{4,1,3,2,0:T(8,128)(2,1)}, u32[]{:S(2)}, u32[]{:S(2)}) %all-to-all-start.3) | async-done | bytes 2097184 | tf_op jit(solution)/shard_map/all_to_all | solution.py:202
  274.8 2.3 convert_reduce_fusion
  281.1 7.3 %psum.35 = f32[2,2048]{1,0:T(2,128)S(1)} all-reduce(f32[2,2048]{1,0:T(2,128)S(1)} %pad_maximum_fusion.3), channel_id=1, replica_groups=mesh['dp_0'=2,'dp_1'=4,'ctx_0'=2,'ctx_1'=8,'ctx_2'=2] {'dp_0'}, use_global_device_ids=true, to_apply=%region_13.14 | all-reduce | flops 4096 | bytes 32768 | tf_op jit(solution)/shard_map/psum | solution.py:53
  288.4 16.9 %psum.36 = f32[2,2048]{1,0:T(2,128)S(1)} all-reduce(f32[2,2048]{1,0:T(2,128)S(1)} %psum.35), channel_id=1, replica_groups=mesh['dp_0'=2,'dp_1'=4,'ctx_0'=2,'ctx_1'=8,'ctx_2'=2] {'dp_1'}, use_global_device_ids=true, to_apply=%region_14.15 | all-reduce | flops 4096 | bytes 32768 | tf_op jit(solution)/shard_map/psum | solution.py:53
  305.3 9.2 %psum.37 = f32[2,2048]{1,0:T(2,128)S(1)} all-reduce(f32[2,2048]{1,0:T(2,128)S(1)} %psum.36), channel_id=1, replica_groups=mesh['dp_0'=2,'dp_1'=4,'ctx_0'=2,'ctx_1'=8,'ctx_2'=2] {'ctx_0'}, use_global_device_ids=true, to_apply=%region_15.16 | all-reduce | flops 4096 | bytes 32768 | tf_op jit(solution)/shard_map/psum | solution.py:53
  314.5 25.4 %psum.38 = f32[2,2048]{1,0:T(2,128)S(1)} all-reduce(f32[2,2048]{1,0:T(2,128)S(1)} %psum.37), channel_id=1, replica_groups=mesh['dp_0'=2,'dp_1'=4,'ctx_0'=2,'ctx_1'=8,'ctx_2'=2] {'ctx_1'}, use_global_device_ids=true, to_apply=%region_16.17 | all-reduce | flops 4096 | bytes 32768 | tf_op jit(solution)/shard_map/psum | solution.py:53
  339.9 3.9 %psum.39 = f32[2,2048]{1,0:T(2,128)} all-reduce(f32[2,2048]{1,0:T(2,128)S(1)} %psum.38), channel_id=1, replica_groups=mesh['dp_0'=2,'dp_1'=4,'ctx_0'=2,'ctx_1'=8,'ctx_2'=2] {'ctx_2'}, use_global_device_ids=true, to_apply=%region_17.18 | all-reduce | flops 4096 | bytes 32768 | tf_op jit(solution)/shard_map/psum | solution.py:53
  (110 shorter events, 23.5 us)
Async XLA Ops:
  0.6 16.3 %copy-start.10 = (bf16[128,2048]{1,0:T(8,128)(2,1)S(1)}, bf16[128,2048]{1,0:T(8,128)(2,1)}, u32[]{:S(2)}) copy-start(bf16[128,2048]{1,0:T(8,128)(2,1)} %param.13) | copy-start | bytes 1572868
  2.0 27.3 %all-to-all-start.1 = ((s32[32,1,128]{2,1,0:T(1,128)}), s32[32,1,128]{2,1,0:T(1,128)S(1)}, u32[]{:S(2)}, u32[]{:S(2)}) async-start(s32[32,1,128]{2,1,0:T(1,128)} %broadcast_in_dim.84), calls=%async_computation.1 | async-start | bytes 32768 | tf_op jit(solution)/shard_map/all_to_all | solution.py:42
  17.0 6.7 %copy-start.6 = (bf16[128,2048]{0,1:T(8,128)(2,1)}, bf16[128,2048]{0,1:T(8,128)(2,1)S(1)}, u32[]{:S(2)}) copy-start(bf16[128,2048]{0,1:T(8,128)(2,1)S(1)} %copy.176) | copy-start | bytes 1572868
  17.0 5.5 %copy-start.11 = (f32[2048]{0:T(1024)S(1)}, f32[2048]{0:T(1024)}, u32[]{:S(2)}) copy-start(f32[2048]{0:T(1024)} %param.15) | copy-start | bytes 24580
  20.5 4.4 %copy-start.12 = (f32[2048]{0:T(1024)S(1)}, f32[2048]{0:T(1024)}, u32[]{:S(2)}) copy-start(f32[2048]{0:T(1024)} %param.16) | copy-start | bytes 24580
  22.5 1.0 copy-start.4
  23.8 1.0 copy-start.2
  29.3 83.2 %all-to-all-start = ((bf16[32,2,192,1,128]{4,2,1,3,0:T(8,128)(2,1)}), bf16[32,2,192,1,128]{4,2,1,3,0:T(8,128)(2,1)S(1)}, u32[]{:S(2)}, u32[]{:S(2)}) async-start(bf16[32,2,192,1,128]{4,2,1,3,0:T(8,128)(2,1)} %pad_maximum_fusion), calls=%async_computation | async-start | bytes 6291456 | tf_op jit(solution)/shard_map/all_to_all | solution.py:27
  112.8 2.6 copy-start.13
  112.8 2.6 copy-start.14
  119.8 3.2 copy-start
  137.7 4.0 %copy-start.1 = (bf16[1024,2048]{1,0:T(8,128)(2,1)S(1)}, bf16[1024,2048]{1,0:T(8,128)(2,1)}, u32[]{:S(2)}) copy-start(bf16[1024,2048]{1,0:T(8,128)(2,1)} %multiply_convert_fusion.4) | copy-start | bytes 12582916 | tf_op jit(solution)/shard_map/while
  150.7 3.2 copy-start
  168.7 4.0 %copy-start.1 = (bf16[1024,2048]{1,0:T(8,128)(2,1)S(1)}, bf16[1024,2048]{1,0:T(8,128)(2,1)}, u32[]{:S(2)}) copy-start(bf16[1024,2048]{1,0:T(8,128)(2,1)} %multiply_convert_fusion.4) | copy-start | bytes 12582916 | tf_op jit(solution)/shard_map/while
  180.6 37.0 %all-to-all-start.2 = ((bf16[32,2,64,1,128]{4,2,3,1,0:T(8,128)(2,1)}), bf16[32,2,64,1,128]{4,2,3,1,0:T(8,128)(2,1)S(1)}, u32[]{:S(2)}, u32[]{:S(2)}) async-start(bf16[32,2,64,1,128]{4,2,3,1,0:T(8,128)(2,1)} %copy.195), calls=%async_computation.2 | async-start | bytes 2097152 | tf_op jit(solution)/shard_map/all_to_all | solution.py:199
  187.2 35.1 %copy-start.3 = (f32[128,2048]{0,1:T(8,128)S(1)}, f32[128,2048]{0,1:T(8,128)}, u32[]{:S(2)}) copy-start(f32[128,2048]{0,1:T(8,128)} %copy-done.2) | copy-start | bytes 3145732
  190.4 33.2 %copy-start.5 = (f32[16,8,16,128]{3,2,1,0:T(8,128)S(1)}, f32[16,8,16,128]{3,2,1,0:T(8,128)}, u32[]{:S(2)}) copy-start(f32[16,8,16,128]{3,2,1,0:T(8,128)} %copy-done.4) | copy-start | bytes 3145732
  217.6 57.2 %all-to-all-start.3 = ((bf16[32,128,2,1,128]{4,1,3,2,0:T(8,128)(2,1)}), bf16[32,128,2,1,128]{4,1,3,2,0:T(8,128)(2,1)}, u32[]{:S(2)}, u32[]{:S(2)}) async-start(bf16[32,128,2,1,128]{4,1,3,2,0:T(8,128)(2,1)} %bitcast.251), calls=%async_computation.3 | async-start | bytes 4194304 | tf_op jit(solution)/shard_map/all_to_all | solution.py:202
  224.5 2.7 copy-start.8
  229.2 48.2 %copy-start.9 = (f32[128,16,128]{2,0,1:T(8,128)S(1)}, f32[128,16,128]{2,0,1:T(8,128)}, u32[]{:S(2)}) copy-start(f32[128,16,128]{2,0,1:T(8,128)} %copy.205) | copy-start | bytes 3145732
  277.2 1.2 copy-start.7
where the time goes:
time: 350 us; the launch traced here: 344 us
  waiting for transfers between devices  146 us (42%)
  blocking collectives  62.8 us (18%)
  matrix products  43 us (12%)
  local copies, waits for them, and re-layouts  36 us (10%)
  starting transfers between devices  32.3 us (9%)
  other arithmetic  22.5 us (6%)
    all_to_all x1, waiting for transfers between devices, in_one_piece(): lax.all_to_all(both, axis, split_axis=split_dim, concat_axis=concat_dim,...  73.1 us
    psum x5, blocking collectives, one_axis_at_a_time(): shard = lax.psum(shard, axis)  62.8 us
    all_to_all x1, waiting for transfers between devices, by_head_groups(): lax.all_to_all(kv_send.astype(jnp.bfloat16), CTX, split_axis=0, concat_ax...  45.7 us
    all_to_all x1, waiting for transfers between devices, by_head_groups(): lax.all_to_all(rows_send.astype(jnp.bfloat16), CTX, split_axis=0, concat_...  27.2 us
    dot_general x2, matrix products, full_attention(): jnp.einsum('qhd,khd->hqk', grads_block, value_block, preferred_element_ty...  14.7 us
    all_to_all x1, starting transfers between devices, sent_to_all(): lax.all_to_all(jnp.broadcast_to(shard[None], (peers, *shard.shape)), axis...  11.4 us
    all_to_all x1, starting transfers between devices, in_one_piece(): lax.all_to_all(both, axis, split_axis=split_dim, concat_axis=concat_dim,...  9.81 us
    unnamed x33, local copies, waits for them, and re-layouts  8.47 us
  transfers between devices with their start and end apart: 4, of which 3 were waited for; matrix products, arithmetic and copies ran while one was open for 7% of the time, Pallas kernels for 0%

commit v1 on v0

v1 whole, which is shorter than its diff:
```python
import functools

import jax
import jax.numpy as jnp
from jax import lax
from jax.experimental import pallas as pl
from jax.experimental.pallas import tpu as pltpu
from jax.sharding import Mesh
from jax.sharding import PartitionSpec as P

HEADS = 16
HEAD = 128
PEERS = ("ctx_0", "ctx_1")
DP_CTX = ("dp_0", "dp_1", "ctx_0", "ctx_1", "ctx_2")
DP = ("dp_0", "dp_1")
EPS = 1e-05
MASKED = -1e30
SCALE = HEAD**-0.5
LOG2E = 1.4426950408889634
F32 = jnp.float32
BF16 = jnp.bfloat16

TOK = 128
MEMBERS = 16
LEN = TOK * MEMBERS
PER = 2
QB = TOK * PER
STEPS = MEMBERS // PER
KC = 256
CHUNKS = LEN // KC


def unit_of(raw):
    values = raw.astype(F32)
    inverse = lax.rsqrt(jnp.mean(values * values, axis=-1, keepdims=True) + EPS)
    return values * inverse, inverse


def norm_back(grad, raw, gain):
    unit, inverse = unit_of(raw)
    u = grad * gain
    projected = jnp.mean(u * unit, axis=-1, keepdims=True)
    part = jnp.sum(grad * unit, axis=0, keepdims=True)
    return (inverse * (u - unit * projected)).astype(BF16), part


def dot(a, b):
    return jnp.dot(a, b, preferred_element_type=F32)


def fold8(x, op):
    return op(x.reshape(x.shape[0] // 8, 8, x.shape[1]), axis=0)


def place_masks(pos_ref, spans, kpos_ref, limit_ref):
    places = pos_ref[...]
    limit = places + 1.0
    for start, end in spans:
        limit = jnp.where((places >= start) & (places < end), end, limit)
    for b in range(STEPS):
        limit_ref[b] = jnp.concatenate(
            [limit[b * PER + i : b * PER + i + 1, :] for i in range(PER)], axis=1
        )
    for r in range(MEMBERS):
        row = jnp.broadcast_to(places[r : r + 1, :], (TOK, TOK))
        kpos_ref[r * TOK : (r + 1) * TOK, :] = row.T


def prepare_keys(k_ref, v_ref, kgain, kn_ref, knT_ref, vT_ref):
    for r in range(MEMBERS):
        rows = slice(r * TOK, (r + 1) * TOK)
        unit, _ = unit_of(k_ref[r])
        normed = unit * kgain
        kn_ref[rows, :] = normed.astype(BF16)
        knT_ref[:, rows] = normed.T.astype(BF16)
        vT_ref[:, rows] = v_ref[r].astype(F32).T.astype(BF16)


def query_step(
    b, q_ref, do_ref, v_ref, qgain, kn_ref, knT_ref, vT_ref, kpos_ref, limit_ref, s_ref, p_ref, dk_ref, dv_ref, gq_ref
):
    raw = q_ref[pl.ds(b * PER, PER)].reshape(QB, HEAD)
    unit, _ = unit_of(raw)
    normed = unit * qgain
    qn = normed.astype(BF16)
    qnT = normed.T.astype(BF16)
    limit = limit_ref[b]
    top = jnp.full((8, QB), MASKED, F32)
    for j in range(CHUNKS):
        rows = slice(j * KC, (j + 1) * KC)
        kp = kpos_ref[rows, :]
        kp = jnp.concatenate([kp] * (QB // 128), axis=1)
        s = jnp.where(kp < limit, dot(kn_ref[rows, :], qnT) * (SCALE * LOG2E), MASKED)
        s_ref[rows, :] = s
        top = jnp.maximum(top, fold8(s, jnp.max))
    top = jnp.max(top, axis=0, keepdims=True)
    total = jnp.zeros((8, QB), F32)
    oT = jnp.zeros((HEAD, QB), F32)
    for j in range(CHUNKS):
        rows = slice(j * KC, (j + 1) * KC)
        p = jnp.exp2(s_ref[rows, :] - top)
        total = total + fold8(p, jnp.sum)
        pb = p.astype(BF16)
        p_ref[rows, :] = pb
        oT = oT + dot(vT_ref[:, rows], pb)
    inv = 1.0 / jnp.sum(total, axis=0, keepdims=True)
    oT = (oT * inv).astype(BF16).astype(F32)
    out = oT.T.astype(BF16)
    gradT = do_ref[pl.ds(b * PER, PER)].reshape(QB, HEAD).astype(F32).T * inv
    gT = gradT.astype(BF16)
    gT32 = gT.astype(F32)
    g = gT32.T.astype(BF16)
    delta = jnp.sum(oT * gT32, axis=0, keepdims=True)
    dqT = jnp.zeros((HEAD, QB), F32)
    for j in range(CHUNKS):
        rows = slice(j * KC, (j + 1) * KC)
        per = KC // TOK
        vj = v_ref[j * per : (j + 1) * per].reshape(KC, HEAD)
        dp = dot(vj, gT)
        pb = p_ref[rows, :]
        ds = (pb.astype(F32) * (dp - delta)).astype(BF16)
        dv_ref[rows, :] += dot(pb, g)
        dk_ref[rows, :] += dot(ds, qn)
        dqT = dqT + dot(knT_ref[:, rows], ds)
    dq = dqT.T * SCALE
    grad, part = norm_back(dq, raw, qgain)
    gq_ref[...] += part
    return out, grad


def local_kernel(
    spans_ref, in_ref, pos_ref, qgain_ref, kgain_ref, out_ref, gains_ref,
    kn_ref, knT_ref, vT_ref, kpos_ref, limit_ref, s_ref, p_ref, dk_ref, dv_ref, gq_ref,
):
    q_ref, k_ref, v_ref, do_ref = (in_ref.at[i] for i in range(4))
    qgain, kgain = qgain_ref[...], kgain_ref[...]
    spans = [
        (spans_ref[0, i].astype(F32), (spans_ref[0, i] + spans_ref[1, i]).astype(F32))
        for i in range(2)
    ]
    place_masks(pos_ref, spans, kpos_ref, limit_ref)
    prepare_keys(k_ref, v_ref, kgain, kn_ref, knT_ref, vT_ref)
    dk_ref[...] = jnp.zeros_like(dk_ref)
    dv_ref[...] = jnp.zeros_like(dv_ref)
    gq_ref[...] = jnp.zeros_like(gq_ref)

    @pl.loop(0, STEPS)
    def _(b):
        out, grad = query_step(
            b, q_ref, do_ref, v_ref, qgain, kn_ref, knT_ref, vT_ref, kpos_ref, limit_ref,
            s_ref, p_ref, dk_ref, dv_ref, gq_ref,
        )
        out_ref[0, pl.ds(b * PER, PER)] = out.reshape(PER, TOK, HEAD)
        out_ref[1, pl.ds(b * PER, PER)] = grad.reshape(PER, TOK, HEAD)

    gk = jnp.zeros((1, HEAD), F32)
    for r in range(MEMBERS):
        rows = slice(r * TOK, (r + 1) * TOK)
        grad, part = norm_back(dk_ref[rows, :] * SCALE, k_ref[r], kgain)
        gk = gk + part
        out_ref[2, r] = grad
        out_ref[3, r] = dv_ref[rows, :].astype(BF16)
    gains_ref[0:1, :] = gq_ref[...]
    gains_ref[1:2, :] = gk


def local_call(spans, packed, places, qgain, kgain):
    vmem = pl.BlockSpec(memory_space=pltpu.VMEM)
    return pl.pallas_call(
        local_kernel,
        out_shape=(
            jax.ShapeDtypeStruct((4, MEMBERS, TOK, HEAD), BF16),
            jax.ShapeDtypeStruct((2, HEAD), F32),
        ),
        in_specs=[pl.BlockSpec(memory_space=pltpu.SMEM)] + [vmem] * 4,
        out_specs=(vmem, vmem),
        scratch_shapes=[
            pltpu.VMEM((LEN, HEAD), BF16),
            pltpu.VMEM((HEAD, LEN), BF16),
            pltpu.VMEM((HEAD, LEN), BF16),
            pltpu.VMEM((LEN, 128), F32),
            pltpu.VMEM((STEPS, 1, QB), F32),
            pltpu.VMEM((LEN, QB), F32),
            pltpu.VMEM((LEN, QB), BF16),
            pltpu.VMEM((LEN, HEAD), F32),
            pltpu.VMEM((LEN, HEAD), F32),
            pltpu.VMEM((1, HEAD), F32),
        ],
        compiler_params=pltpu.CompilerParams(vmem_limit_bytes=40 << 20),
    )(spans, packed, places, qgain, kgain)


def body(query_rows, key_rows, value_rows, cotangent, query_gain, key_gain, positions, span_start, span_length):
    rows = query_rows.shape[0]
    core = lax.axis_index("ctx_2")
    head = lax.axis_index(PEERS)
    packed = jnp.stack(
        [t.reshape(rows, HEADS, HEAD).transpose(1, 0, 2) for t in (query_rows, key_rows, value_rows, cotangent)],
        axis=0,
    )
    packed = lax.all_to_all(packed, PEERS, split_axis=1, concat_axis=1, tiled=True)
    places = lax.all_gather(positions, PEERS).astype(F32)
    spans = jnp.stack(
        [lax.dynamic_index_in_dim(t, core, 0, keepdims=False) for t in (span_start, span_length)]
    )
    pick = lambda g: lax.dynamic_index_in_dim(g.reshape(HEADS, HEAD), head, 0, keepdims=True)
    outs, gains = local_call(spans, packed, places, pick(query_gain), pick(key_gain))
    outs = lax.all_to_all(outs, PEERS, split_axis=1, concat_axis=1, tiled=True)
    outs = [outs[i].transpose(1, 0, 2).reshape(rows, HEADS * HEAD) for i in range(4)]
    slots = (jnp.arange(HEADS) == head)[None, :, None]
    gain_grads = jnp.where(slots, gains[:, None, :], 0.0).reshape(2, HEADS * HEAD)
    gain_grads = lax.psum(gain_grads, DP_CTX)
    return (*outs, gain_grads)


def solution(mesh):
    split = Mesh(mesh.devices.reshape(2, 4, 2, 8, 2), DP_CTX)
    rows = P(DP_CTX, None)
    return jax.shard_map(
        body,
        mesh=split,
        in_specs=(rows, rows, rows, rows, P(), P(), P(DP_CTX), P(DP, None), P(DP, None)),
        out_specs=(rows, rows, rows, rows, P()),
        check_vma=False,
    )
```

time: 350 us -> 227 us (0.65); the launches traced: 344 us -> 226 us
  waiting for transfers between devices: 146 us -> 0.01 us
  blocking collectives: 62.8 us -> 164 us
  matrix products: 43 us -> 0 us
  Pallas kernels: 0 us -> 26 us
  other arithmetic: 22.5 us -> 1.5 us
  local copies, waits for them, and re-layouts: 36 us -> 17.3 us
  starting transfers between devices: 32.3 us -> 16.5 us
    all_to_all x4 -> x2, waiting for transfers between devices: 146 us -> 0.01 us  [the longest x1 0.01 us: body(): lax.all_to_all(packed, PEERS, split_axis=1, concat_axis=1, tiled=True)]
    all_gather x0 -> x1, blocking collectives: none -> 78.7 us  [body(): places = lax.all_gather(positions, PEERS).astype(F32)]
    dot_general x12 -> x0, matrix products: 43 us -> none  [the longest x2 14.7 us: full_attention(): jnp.einsum('qhd,khd->hqk', grads_block, value_block, preferred_element_ty...]
    pallas_call x0 -> x1, Pallas kernels: none -> 26 us  [local_call(): pl.pallas_call(local_kernel, out_shape=(jax.ShapeDtypeStruct((4, MEMBERS,...]
    psum x5 -> x1, blocking collectives: 62.8 us -> 85 us  [body(): gain_grads = lax.psum(gain_grads, DP_CTX)]
    all_to_all x4 -> x2, starting transfers between devices: 32.3 us -> 16.5 us  [the longest x1 11.3 us: body(): lax.all_to_all(packed, PEERS, split_axis=1, concat_axis=1, tiled=True)]
    reduce_sum x11 -> x0, other arithmetic: 8.45 us -> none  [the longest x2 2.51 us: full_attention(): jnp.sum(jnp.exp(scores - row_max), axis=-1, keepdims=True)]
    dynamic_update_slice x10 -> x0, local copies, waits for them, and re-layouts: 5.76 us -> none  [by_head_groups(): lax.map(full_attention, (query_pack, key_pack, query_places, key_places,...]
  transfers between devices with their start and end apart: 4 -> 2, of which waited for: 3 -> 0; matrix products, arithmetic and copies ran while one was open for 7% -> 0% of each run, Pallas kernels for 0% -> 0%
where the time goes in v1:
time: 227 us; the launch traced here: 226 us
  blocking collectives  164 us (72%)
  Pallas kernels  26 us (11%)
  local copies, waits for them, and re-layouts  17.3 us (8%)
  starting transfers between devices  16.5 us (7%)
    psum x1, blocking collectives, body(): gain_grads = lax.psum(gain_grads, DP_CTX)  85 us
    all_gather x1, blocking collectives, body(): places = lax.all_gather(positions, PEERS).astype(F32)  78.7 us
    pallas_call x1, Pallas kernels, local_call(): pl.pallas_call(local_kernel, out_shape=(jax.ShapeDtypeStruct((4, MEMBERS,...  26 us
    all_to_all x1, starting transfers between devices, body(): lax.all_to_all(packed, PEERS, split_axis=1, concat_axis=1, tiled=True)  11.3 us
    unnamed x25, local copies, waits for them, and re-layouts  11 us
    all_to_all x1, starting transfers between devices, body(): outs = lax.all_to_all(outs, PEERS, split_axis=1, concat_axis=1, tiled=True)  5.12 us
  transfers between devices with their start and end apart: 2, of which 0 were waited for; matrix products, arithmetic and copies ran while one was open for 0% of the time, Pallas kernels for 0%

profile of v1, /device:TPU:32, one launch (start us, length us, event | category | flops | bytes accessed | tf_op | source)
XLA Modules:
  0.0 225.7 jit_solution(8781674575273936171)
XLA Ops:
  0.6 0.0 copy-start.1
  0.6 0.0 copy-start.2
  0.7 1.4 copy.35
  2.1 1.3 copy.34
  3.4 0.0 copy-done.1
  3.4 1.0 copy.33
  4.4 0.0 copy-done.2
  4.4 1.0 copy.32
  5.4 1.5 pad_maximum_fusion
  6.9 2.6 %copy.36 = bf16[4,16,128,128]{3,2,0,1:T(8,128)(2,1)} copy(bf16[4,16,128,128]{2,3,1,0:T(8,128)(2,1)S(1)} %pad_maximum_fusion) | data formatting | bytes 4194304 | tf_op jit(solution)/shard_map/stack | solution.py:197
  9.5 0.0 copy-start.3
  9.5 0.0 copy-start.4
  9.5 0.0 copy-start.5
  9.5 11.3 %all-to-all-start = ((bf16[4,16,128,128]{3,2,0,1:T(8,128)(2,1)}), bf16[4,16,128,128]{3,2,0,1:T(8,128)(2,1)S(1)}, u32[]{:S(2)}, u32[]{:S(2)}) async-start(bf16[4,16,128,128]{3,2,0,1:T(8,128)(2,1)} %copy.36), calls=%async_computation | async-start | bytes 4194304 | tf_op jit(solution)/shard_map/all_to_all | solution.py:201
  20.8 0.0 copy-done.3
  20.8 78.7 %all-gather.1 = s32[16,1,128]{2,1,0:T(1,128)S(1)} all-gather(s32[1,1,128]{2,1,0:T(1,128)S(1)} %bitcast.61), channel_id=2, replica_groups=mesh['dp_0'=2,'dp_1'=4,'ctx_0'=2,'ctx_1'=8,'ctx_2'=2] {'ctx_0','ctx_1'}, dimensions={0}, use_global_device_ids=true | all-gather | bytes 8704 | tf_op jit(solution)/shard_map/all_gather | solution.py:202
  99.5 0.0 copy-done.4
  99.5 0.0 copy-done.5
  99.5 0.7 constant_dynamic-slice_fusion
  100.3 0.0 all-to-all-done
  100.3 0.1 copy.38.in_ref
  100.4 26.0 %shard_map.128 = (bf16[4,16,128,128]{3,2,1,0:T(8,128)(2,1)S(1)}, f32[2,128]{1,0:T(2,128)S(1)}) custom-call(s32[2,2]{1,0:T(2,128)S(1)} %pad_add_fusion.spans_ref, bf16[4,16,128,128]{3,2,1,0:T(8,128)(2,1)S(1)} %copy.38.in_ref, f32[16,128]{1,0:T(8,128)S(1)} %convert_bitcast_fusion.pos_ref, f32[1,128]{1,0:T(1,128)S(1)} %get-tuple-element.26.qgain_ref, ...), custom_call_target="tpu_custom_call" | custom-call | tf_op jit(solution)/shard_map/pallas_call | solution.py:169
  126.5 1.6 copy.39
  128.0 5.1 %all-to-all-start.1 = ((bf16[4,16,128,128]{3,2,0,1:T(8,128)(2,1)}), bf16[4,16,128,128]{3,2,0,1:T(8,128)(2,1)S(1)}, u32[]{:S(2)}, u32[]{:S(2)}) async-start(bf16[4,16,128,128]{3,2,0,1:T(8,128)(2,1)} %copy.39), calls=%async_computation.1 | async-start | bytes 4194304 | tf_op jit(solution)/shard_map/all_to_all | solution.py:208
  133.2 0.1 broadcast_bitcast_fusion.1
  133.3 85.0 %psum.7 = f32[2,2048]{1,0:T(2,128)} all-reduce(f32[2,2048]{1,0:T(2,128)S(1)} %bitcast_select_fusion), channel_id=1, replica_groups=mesh['dp_0'=2,'dp_1'=4,'ctx_0'=2,'ctx_1'=8,'ctx_2'=2] {'dp_0','dp_1','ct..., use_global_device_ids=true, to_apply=%region_0.1 | all-reduce | flops 4096 | bytes 32768 | tf_op jit(solution)/shard_map/psum | solution.py:212
  218.3 0.0 all-to-all-done.1
  218.3 1.2 fusion
  219.5 0.0 copy-start
  219.5 1.4 copy.48
  220.8 1.0 copy.44
  221.8 0.0 copy-done
  221.9 0.3 copy.49
  222.1 1.0 copy.45
  223.2 0.3 copy.50
  223.4 1.0 copy.46
  224.4 0.3 copy.51
  224.7 1.0 copy.47
  (6 shorter events, 0.0 us)
Async XLA Ops:
  0.6 2.7 %copy-start.1 = (bf16[128,2048]{1,0:T(8,128)(2,1)S(1)}, bf16[128,2048]{1,0:T(8,128)(2,1)}, u32[]{:S(2)}) copy-start(bf16[128,2048]{1,0:T(8,128)(2,1)} %param.10) | copy-start | bytes 1572868
  0.6 3.7 %copy-start.2 = (bf16[128,2048]{1,0:T(8,128)(2,1)S(1)}, bf16[128,2048]{1,0:T(8,128)(2,1)}, u32[]{:S(2)}) copy-start(bf16[128,2048]{1,0:T(8,128)(2,1)} %param.9) | copy-start | bytes 1572868
  9.5 11.4 %copy-start.3 = (s32[128]{0:T(128)S(1)}, s32[128]{0:T(128)}, u32[]{:S(2)}) copy-start(s32[128]{0:T(128)} %param.15) | copy-start | bytes 1540
  9.5 90.1 %copy-start.4 = (s32[2,2]{1,0:T(2,128)S(1)}, s32[2,2]{1,0:T(2,128)}, u32[]{:S(2)}) copy-start(s32[2,2]{1,0:T(2,128)} %param.17) | copy-start | bytes 52
  9.5 90.1 %copy-start.5 = (s32[2,2]{1,0:T(2,128)S(1)}, s32[2,2]{1,0:T(2,128)}, u32[]{:S(2)}) copy-start(s32[2,2]{1,0:T(2,128)} %param.16) | copy-start | bytes 52
  9.5 90.8 %all-to-all-start = ((bf16[4,16,128,128]{3,2,0,1:T(8,128)(2,1)}), bf16[4,16,128,128]{3,2,0,1:T(8,128)(2,1)S(1)}, u32[]{:S(2)}, u32[]{:S(2)}) async-start(bf16[4,16,128,128]{3,2,0,1:T(8,128)(2,1)} %copy.36), calls=%async_computation | async-start | bytes 4194304 | tf_op jit(solution)/shard_map/all_to_all | solution.py:201
  128.0 90.3 %all-to-all-start.1 = ((bf16[4,16,128,128]{3,2,0,1:T(8,128)(2,1)}), bf16[4,16,128,128]{3,2,0,1:T(8,128)(2,1)S(1)}, u32[]{:S(2)}, u32[]{:S(2)}) async-start(bf16[4,16,128,128]{3,2,0,1:T(8,128)(2,1)} %copy.39), calls=%async_computation.1 | async-start | bytes 4194304 | tf_op jit(solution)/shard_map/all_to_all | solution.py:208
  219.5 2.4 %copy-start = (bf16[1,16,128,128]{3,2,0,1:T(8,128)(2,1)S(1)}, bf16[1,16,128,128]{3,2,0,1:T(8,128)(2,1)}, u32[]{:S(2)}) copy-start(bf16[1,16,128,128]{3,2,0,1:T(8,128)(2,1)} %get-tuple-element.21) | copy-start | bytes 1572868

commit v2 on v1

v2 whole, which is shorter than its diff:
```python
import jax
import jax.numpy as jnp
from jax import lax
from jax.experimental import pallas as pl
from jax.experimental.pallas import tpu as pltpu
from jax.sharding import Mesh
from jax.sharding import PartitionSpec as P

HEADS = 16
HEAD = 128
DP_CTX = ("dp_0", "dp_1", "ctx_0", "ctx_1", "ctx_2")
DP = ("dp_0", "dp_1")
EPS = 1e-05
MASKED = -1e30
SCALE = HEAD**-0.5
LOG2E = 1.4426950408889634
MESH = pl.DeviceIdType.MESH
F32 = jnp.float32
BF16 = jnp.bfloat16

TOK = 128
MEMBERS = 16
LEN = TOK * MEMBERS
PER = 2
QB = TOK * PER
STEPS = MEMBERS // PER
KC = 256
CHUNKS = LEN // KC


def unit_of(raw):
    values = raw.astype(F32)
    inverse = lax.rsqrt(jnp.mean(values * values, axis=-1, keepdims=True) + EPS)
    return values * inverse, inverse


def norm_back(grad, raw, gain):
    unit, inverse = unit_of(raw)
    u = grad * gain
    projected = jnp.mean(u * unit, axis=-1, keepdims=True)
    part = jnp.sum(grad * unit, axis=0, keepdims=True)
    return (inverse * (u - unit * projected)).astype(BF16), part


def dot(a, b):
    return jnp.dot(a, b, preferred_element_type=F32)


def fold8(x, op):
    return op(x.reshape(x.shape[0] // 8, 8, x.shape[1]), axis=0)


def prepare_key(n, k_ref, kgain, kn_ref, knT_ref):
    rows = pl.ds(pl.multiple_of(n * TOK, TOK), TOK)
    unit, _ = unit_of(k_ref[n])
    normed = unit * kgain
    kn_ref[rows, :] = normed.astype(BF16)
    knT_ref[:, rows] = normed.T.astype(BF16)


def prepare_value(n, v_ref, vT_ref):
    rows = pl.ds(pl.multiple_of(n * TOK, TOK), TOK)
    vT_ref[:, rows] = v_ref[n].astype(F32).T.astype(BF16)


def query_step(
    b, q_ref, do_ref, v_ref, qgain, kn_ref, knT_ref, vT_ref, kpos_ref, limit_ref, s_ref, p_ref, dk_ref, dv_ref, gq_ref
):
    raw = q_ref[pl.ds(b * PER, PER)].reshape(QB, HEAD)
    unit, _ = unit_of(raw)
    normed = unit * qgain
    qn = normed.astype(BF16)
    qnT = normed.T.astype(BF16)
    limit = limit_ref[b]
    top = jnp.full((8, QB), MASKED, F32)
    for j in range(CHUNKS):
        rows = slice(j * KC, (j + 1) * KC)
        kp = kpos_ref[rows, :]
        kp = jnp.concatenate([kp] * (QB // 128), axis=1)
        s = jnp.where(kp < limit, dot(kn_ref[rows, :], qnT) * (SCALE * LOG2E), MASKED)
        s_ref[rows, :] = s
        top = jnp.maximum(top, fold8(s, jnp.max))
    top = jnp.max(top, axis=0, keepdims=True)
    total = jnp.zeros((8, QB), F32)
    oT = jnp.zeros((HEAD, QB), F32)
    for j in range(CHUNKS):
        rows = slice(j * KC, (j + 1) * KC)
        p = jnp.exp2(s_ref[rows, :] - top)
        total = total + fold8(p, jnp.sum)
        pb = p.astype(BF16)
        p_ref[rows, :] = pb
        oT = oT + dot(vT_ref[:, rows], pb)
    inv = 1.0 / jnp.sum(total, axis=0, keepdims=True)
    oT = (oT * inv).astype(BF16).astype(F32)
    out = oT.T.astype(BF16)
    gradT = do_ref[pl.ds(b * PER, PER)].reshape(QB, HEAD).astype(F32).T * inv
    gT = gradT.astype(BF16)
    gT32 = gT.astype(F32)
    g = gT32.T.astype(BF16)
    delta = jnp.sum(oT * gT32, axis=0, keepdims=True)
    dqT = jnp.zeros((HEAD, QB), F32)
    for j in range(CHUNKS):
        rows = slice(j * KC, (j + 1) * KC)
        per = KC // TOK
        vj = v_ref[j * per : (j + 1) * per].reshape(KC, HEAD)
        dp = dot(vj, gT)
        pb = p_ref[rows, :]
        ds = (pb.astype(F32) * (dp - delta)).astype(BF16)
        dv_ref[rows, :] += dot(pb, g)
        dk_ref[rows, :] += dot(ds, qn)
        dqT = dqT + dot(knT_ref[:, rows], ds)
    dq = dqT.T * SCALE
    grad, part = norm_back(dq, raw, qgain)
    gq_ref[...] += part
    return out, grad


def across(step):
    return lax.rem(8 + lax.div(step + 1, 2) * (2 * lax.rem(step, 2) - 1), 8)


def device(y, z):
    return {"ctx_0": y, "ctx_1": z}


def columns(head):
    return pl.ds(pl.multiple_of(head * HEAD, HEAD), HEAD)


def fused_kernel(
    start_ref, length_ref, q_hbm, k_hbm, v_hbm, do_hbm, place_ref, qgain_ref, kgain_ref,
    out_hbm, gq_hbm, gk_hbm, gv_hbm, gains_ref,
    recv, places, send, kn_ref, knT_ref, vT_ref, kpos_ref, limit_ref, s_ref, p_ref, dk_ref, dv_ref, gq_ref,
    part_ref, parts, whole_ref, wholes, in_send, in_recv, back_send, back_recv, gain_send, gain_recv,
):
    y, z, core = lax.axis_index("ctx_0"), lax.axis_index("ctx_1"), lax.axis_index("ctx_2")
    d0, d1 = lax.axis_index("dp_0"), lax.axis_index("dp_1")
    me = y * 8 + z
    member = d0 * 8 + d1 * 2 + core

    def target(n):
        return lax.rem(y + lax.rem(n, 2), 2), lax.rem(z + across(lax.div(n, 2)), 8)

    def origin(n):
        return lax.rem(y + lax.rem(n, 2), 2), lax.rem(z + 8 - across(lax.div(n, 2)), 8)

    def sibling(t):
        return {
            "dp_0": lax.rem(d0 + t // 8, 2),
            "dp_1": lax.rem(d1 + t // 2 % 4, 4),
            "ctx_2": lax.rem(core + t % 2, 2),
        }

    targets = [target(jnp.int32(n)) for n in range(MEMBERS)]
    barrier = pltpu.get_barrier_semaphore()
    for n in range(1, MEMBERS):
        pl.semaphore_signal(barrier, inc=1, device_id=device(*targets[n]), device_id_type=MESH)
        pl.semaphore_signal(barrier, inc=1, device_id=sibling(n), device_id_type=MESH)
    pl.semaphore_wait(barrier, 2 * (MEMBERS - 1))

    def incoming(a, n, at):
        if a == 4:
            source, dest = place_ref, places.at[n]
        else:
            source, dest = (q_hbm, k_hbm, v_hbm, do_hbm)[a], recv.at[a, n]
            source = source.at[:, columns(at[0] * 8 + at[1])]
        return source, dest

    def arrival(a, n, at):
        source, dest = incoming(a, n, at)
        return pltpu.make_async_remote_copy(
            source, dest, in_send.at[a, n], in_recv.at[a, n], device_id=device(*at), device_id_type=MESH
        )

    def own(a):
        source, dest = incoming(a, 0, (y, z))
        return pltpu.make_async_copy(source, dest, in_recv.at[a, 0])

    for group in ((4,), (1,), (2,), (0, 3)):
        for a in group:
            own(a).start()
        for n in range(1, MEMBERS):
            for a in group:
                arrival(a, n, targets[n]).start()

    qgain, kgain = qgain_ref[pl.ds(me, 1), :], kgain_ref[pl.ds(me, 1), :]
    dk_ref[...] = jnp.zeros_like(dk_ref)
    dv_ref[...] = jnp.zeros_like(dv_ref)
    gq_ref[...] = jnp.zeros_like(gq_ref)
    part_ref[...] = jnp.zeros_like(part_ref)
    spans = []
    for i in range(2):
        first = start_ref[core, i]
        spans.append((first.astype(F32), (first + length_ref[core, i]).astype(F32)))

    own(4).wait()
    for n in range(1, MEMBERS):
        arrival(4, n, targets[n]).wait_recv()
    for n in range(MEMBERS):
        row = places[n]
        limit = row + 1.0
        for start, end in spans:
            limit = jnp.where((row >= start) & (row < end), end, limit)
        limit_ref[n // PER, :, n % PER * TOK : (n % PER + 1) * TOK] = limit
        kpos_ref[n * TOK : (n + 1) * TOK, :] = jnp.broadcast_to(row, (TOK, TOK)).T

    own(1).wait()
    prepare_key(0, recv.at[1], kgain, kn_ref, knT_ref)

    @pl.loop(1, MEMBERS)
    def _(n):
        arrival(1, n, (y, z)).wait_recv()
        prepare_key(n, recv.at[1], kgain, kn_ref, knT_ref)

    own(2).wait()
    prepare_value(0, recv.at[2], vT_ref)

    @pl.loop(1, MEMBERS)
    def _(n):
        arrival(2, n, (y, z)).wait_recv()
        prepare_value(n, recv.at[2], vT_ref)

    outs = (out_hbm, gq_hbm, gk_hbm, gv_hbm)

    def back(i, n, at, head):
        return pltpu.make_async_remote_copy(
            send.at[i, n], outs[i].at[:, columns(head)], back_send.at[i, n], back_recv.at[i, n],
            device_id=device(*at), device_id_type=MESH,
        )

    def stays(i):
        return pltpu.make_async_copy(send.at[i, 0], outs[i].at[:, columns(me)], back_send.at[i, 0])

    def send_step(b):
        for j in range(PER):
            n = b * PER + j
            if j == 0:

                @pl.when(b == 0)
                def _():
                    stays(0).start()
                    stays(1).start()

                @pl.when(b > 0)
                def _():
                    back(0, n, origin(n), me).start()
                    back(1, n, origin(n), me).start()

            else:
                back(0, n, origin(n), me).start()
                back(1, n, origin(n), me).start()

    own(0).wait()
    own(3).wait()

    @pl.loop(0, STEPS)
    def _(b):
        @pl.when(b > 0)
        def _():
            arrival(0, b * PER, (y, z)).wait_recv()
            arrival(3, b * PER, (y, z)).wait_recv()

        for j in range(1, PER):
            arrival(0, b * PER + j, (y, z)).wait_recv()
            arrival(3, b * PER + j, (y, z)).wait_recv()
        out, grad = query_step(
            b, recv.at[0], recv.at[3], recv.at[2], qgain, kn_ref, knT_ref, vT_ref, kpos_ref, limit_ref,
            s_ref, p_ref, dk_ref, dv_ref, gq_ref,
        )
        send[0, pl.ds(b * PER, PER)] = out.reshape(PER, TOK, HEAD)
        send[1, pl.ds(b * PER, PER)] = grad.reshape(PER, TOK, HEAD)

        @pl.when(b > 0)
        def _():
            send_step(b - 1)

    for n in range(MEMBERS):
        send[3, n] = dv_ref[n * TOK : (n + 1) * TOK, :].astype(BF16)
    send_step(jnp.int32(STEPS - 1))
    gk = jnp.zeros((1, HEAD), F32)
    for n in range(MEMBERS):
        grad, part = norm_back(dk_ref[n * TOK : (n + 1) * TOK, :] * SCALE, recv[1, n], kgain)
        gk = gk + part
        send[2, n] = grad
        if n == 0:
            part_ref[0:1, :] = gq_ref[...]
            stays(3).start()
        else:
            back(3, n, origin(jnp.int32(n)), me).start()
    part_ref[1:2, :] = gk
    parts[member] = part_ref[...]

    def half(n):
        if n == 0:
            stays(2).start()
        else:
            back(2, n, origin(jnp.int32(n)), me).start()

    def spread(t):
        return pltpu.make_async_remote_copy(
            part_ref, parts.at[member], gain_send.at[0, t], gain_recv.at[0, t],
            device_id=sibling(t), device_id_type=MESH,
        )

    def publish(n):
        return pltpu.make_async_remote_copy(
            whole_ref, wholes.at[me], gain_send.at[1, n], gain_recv.at[1, n],
            device_id=device(*targets[n]), device_id_type=MESH,
        )

    for n in range(4):
        half(n)
    for t in range(1, MEMBERS):
        spread(t).start()
    for n in range(4, 8):
        half(n)
    for t in range(1, MEMBERS):
        spread(t).wait_recv()
    whole = parts[0]
    for t in range(1, MEMBERS):
        whole = whole + parts[t]
    whole_ref[...] = whole
    wholes[me] = whole
    for n in range(8, 12):
        half(n)
    for n in range(1, MEMBERS):
        publish(n).start()
    for n in range(12, MEMBERS):
        half(n)
    for n in range(1, MEMBERS):
        publish(n).wait_recv()
    for h in range(HEADS):
        gains_ref[:, h * HEAD : (h + 1) * HEAD] = wholes[h, 0:2, :]

    for n in range(1, MEMBERS):
        spread(n).wait_send()
        publish(n).wait_send()
        for a in range(5):
            arrival(a, n, targets[n]).wait_send()
    for i in range(4):
        stays(i).wait()
    for n in range(1, MEMBERS):
        yy, zz = targets[n]
        for i in range(4):
            back(i, n, (yy, zz), yy * 8 + zz).wait()


def body(query_rows, key_rows, value_rows, cotangent, query_gain, key_gain, positions, span_start, span_length):
    rows = query_rows.shape[0]
    vmem = pl.BlockSpec(memory_space=pltpu.VMEM)
    smem = pl.BlockSpec(memory_space=pltpu.SMEM)
    hbm = pl.BlockSpec(memory_space=pl.ANY)
    row_array = jax.ShapeDtypeStruct((rows, HEADS * HEAD), BF16)
    dma = pltpu.SemaphoreType.DMA
    return pl.pallas_call(
        fused_kernel,
        out_shape=(row_array,) * 4 + (jax.ShapeDtypeStruct((2, HEADS * HEAD), F32),),
        in_specs=[smem] * 2 + [hbm] * 4 + [vmem] * 3,
        out_specs=(hbm,) * 4 + (vmem,),
        scratch_shapes=[
            pltpu.VMEM((4, MEMBERS, TOK, HEAD), BF16),
            pltpu.VMEM((MEMBERS, 1, TOK), F32),
            pltpu.VMEM((4, MEMBERS, TOK, HEAD), BF16),
            pltpu.VMEM((LEN, HEAD), BF16),
            pltpu.VMEM((HEAD, LEN), BF16),
            pltpu.VMEM((HEAD, LEN), BF16),
            pltpu.VMEM((LEN, 128), F32),
            pltpu.VMEM((STEPS, 1, QB), F32),
            pltpu.VMEM((LEN, QB), F32),
            pltpu.VMEM((LEN, QB), BF16),
            pltpu.VMEM((LEN, HEAD), F32),
            pltpu.VMEM((LEN, HEAD), F32),
            pltpu.VMEM((1, HEAD), F32),
            pltpu.VMEM((8, HEAD), F32),
            pltpu.VMEM((MEMBERS, 8, HEAD), F32),
            pltpu.VMEM((8, HEAD), F32),
            pltpu.VMEM((MEMBERS, 8, HEAD), F32),
            dma((5, MEMBERS)),
            dma((5, MEMBERS)),
            dma((4, MEMBERS)),
            dma((4, MEMBERS)),
            dma((2, MEMBERS)),
            dma((2, MEMBERS)),
        ],
        compiler_params=pltpu.CompilerParams(
            collective_id=0, has_side_effects=True, vmem_limit_bytes=40 << 20
        ),
    )(
        span_start, span_length, query_rows, key_rows, value_rows, cotangent,
        positions.astype(F32).reshape(1, TOK), query_gain.reshape(HEADS, HEAD), key_gain.reshape(HEADS, HEAD),
    )


def solution(mesh):
    split = Mesh(mesh.devices.reshape(2, 4, 2, 8, 2), DP_CTX)
    rows = P(DP_CTX, None)
    return jax.shard_map(
        body,
        mesh=split,
        in_specs=(rows, rows, rows, rows, P(), P(), P(DP_CTX), P(DP, None), P(DP, None)),
        out_specs=(rows, rows, rows, rows, P()),
        check_vma=False,
    )
```

time: 227 us -> 121 us (0.53)
  blocking collectives: 164 us -> 0 us
  Pallas kernels: 26 us -> 109 us
  starting transfers between devices: 16.5 us -> 0 us
  local copies, waits for them, and re-layouts: 17.3 us -> 10.7 us
    psum x1 -> x0, blocking collectives: 85 us -> none  [body(): gain_grads = lax.psum(gain_grads, DP_CTX)]
    pallas_call x1, Pallas kernels: 26 us -> 109 us  [body(): pl.pallas_call(fused_kernel, out_shape=(row_array,) * 4 + (jax.ShapeDtype...]
    all_gather x1 -> x0, blocking collectives: 78.7 us -> none  [body(): places = lax.all_gather(positions, PEERS).astype(F32)]
    all_to_all x2 -> x0, starting transfers between devices: 16.5 us -> none  [the longest x1 11.3 us: body(): lax.all_to_all(packed, PEERS, split_axis=1, concat_axis=1, tiled=True)]
    another operation x1 -> x0, local copies, waits for them, and re-layouts: 2.61 us -> none  [body(): jnp.stack([t.reshape(rows, HEADS, HEAD).transpose(1, 0, 2) for t in (quer...]
    unnamed x25 -> x23, local copies, waits for them, and re-layouts: 11 us -> 10.7 us
  transfers between devices with their start and end apart: 2 -> 0, of which waited for: 0 -> 0; matrix products, arithmetic and copies ran while one was open for 0% -> 0% of each run, Pallas kernels for 0% -> 0%
where the time goes in v2:
time: 121 us; the launch traced here: 120 us
  Pallas kernels  109 us (90%)
  local copies, waits for them, and re-layouts  10.7 us (9%)
    pallas_call x1, Pallas kernels, body(): pl.pallas_call(fused_kernel, out_shape=(row_array,) * 4 + (jax.ShapeDtype...  109 us
    unnamed x23, local copies, waits for them, and re-layouts  10.7 us

profile of v2, /device:TPU:32, one launch (start us, length us, event | category | flops | bytes accessed | tf_op | source)
XLA Modules:
  0.0 120.4 jit_solution(17321386536002628503)
XLA Ops:
  0.6 0.0 copy-start.8
  0.6 0.0 copy-start.7
  0.7 0.6 copy-done.8
  1.3 0.0 copy-start.6
  1.3 0.0 copy-done.7
  1.3 0.6 copy-done.6
  2.0 0.0 copy-start
  2.0 1.0 copy-done
  3.0 0.0 copy-start.1
  3.0 1.0 copy-done.1
  4.1 0.0 copy-start.2
  4.1 1.0 copy-done.2
  5.1 0.0 copy-start.3
  5.1 1.0 copy-done.3
  6.1 0.0 copy-start.4
  6.1 0.7 copy-done.4
  6.8 0.0 copy-start.5
  6.8 0.7 copy-done.5
  7.5 109.1 %shard_map.128 = (bf16[128,2048]{1,0:T(8,128)(2,1)S(1)}, bf16[128,2048]{1,0:T(8,128)(2,1)S(1)}, bf16[128,2048]{1,0:T(8,128)(2,1)S(1)}, bf16[128,2048]{1,0:T(8,128)(2,1)S(1)}, f32[2,2048]{1,0:T(2,128)S(1)}) custom-call(s32[2,2]{1,0:T(2,128)S(1)} %copy-done.6, s32[2,2]{1,0:T(2,128)S(1)} %copy-done.7, bf16[128,2048]{1,0:T(8,128)(2,1)S(1)} %copy-done, ...), custom_call_target="tpu_custom_call" | custom-call | tf_op jit(solution)/shard_map/pallas_call | solution.py:355
  116.6 0.8 copy.19
  117.4 0.8 copy.20
  118.2 0.8 copy.21
  119.0 0.8 copy.22
  119.8 0.6 copy.23
  (1 shorter events, 0.0 us)
Async XLA Ops:
  0.6 0.7 copy-start.8
  0.6 0.7 copy-start.7
  1.3 0.7 copy-start.6
  2.0 1.0 copy-start
  3.0 1.0 copy-start.1
  4.1 1.0 copy-start.2
  5.1 1.0 copy-start.3
  6.1 0.7 copy-start.4
  6.8 0.7 copy-start.5

commit v3 on v2

--- a/solution.py
+++ b/solution.py
@@ -18,6 +18,8 @@
 F32 = jnp.float32
 BF16 = jnp.bfloat16
 
+SEQS = 2
+SPANS = 2
 TOK = 128
 MEMBERS = 16
 LEN = TOK * MEMBERS
@@ -26,6 +28,7 @@
 STEPS = MEMBERS // PER
 KC = 256
 CHUNKS = LEN // KC
+GRANT = 40 << 20
 
 
 def unit_of(raw):
@@ -128,10 +131,10 @@
 
 
 def fused_kernel(
-    start_ref, length_ref, q_hbm, k_hbm, v_hbm, do_hbm, place_ref, qgain_ref, kgain_ref,
+    start_hbm, length_hbm, q_hbm, k_hbm, v_hbm, do_hbm, place_ref, qgain_hbm, kgain_hbm,
     out_hbm, gq_hbm, gk_hbm, gv_hbm, gains_ref,
     recv, places, send, kn_ref, knT_ref, vT_ref, kpos_ref, limit_ref, s_ref, p_ref, dk_ref, dv_ref, gq_ref,
-    part_ref, parts, whole_ref, wholes, in_send, in_recv, back_send, back_recv, gain_send, gain_recv,
+    part_ref, parts, whole_ref, wholes, start_ref, length_ref, qgain_ref, kgain_ref, small, in_send, in_recv, back_send, back_recv, gain_send, gain_recv,
 ):
     y, z, core = lax.axis_index("ctx_0"), lax.axis_index("ctx_1"), lax.axis_index("ctx_2")
     d0, d1 = lax.axis_index("dp_0"), lax.axis_index("dp_1")
@@ -156,6 +159,23 @@
     for n in range(1, MEMBERS):
         pl.semaphore_signal(barrier, inc=1, device_id=device(*targets[n]), device_id_type=MESH)
         pl.semaphore_signal(barrier, inc=1, device_id=sibling(n), device_id_type=MESH)
+    fetches = [
+        pltpu.make_async_copy(source, dest, small.at[i])
+        for i, (source, dest) in enumerate(
+            (
+                (start_hbm, start_ref),
+                (length_hbm, length_ref),
+                (qgain_hbm.at[pl.ds(me, 1), :], qgain_ref),
+                (kgain_hbm.at[pl.ds(me, 1), :], kgain_ref),
+            )
+        )
+    ]
+    for fetch in fetches:
+        fetch.start()
+    dk_ref[...] = jnp.zeros_like(dk_ref)
+    dv_ref[...] = jnp.zeros_like(dv_ref)
+    gq_ref[...] = jnp.zeros_like(gq_ref)
+    part_ref[...] = jnp.zeros_like(part_ref)
     pl.semaphore_wait(barrier, 2 * (MEMBERS - 1))
 
     def incoming(a, n, at):
@@ -183,11 +203,9 @@
             for a in group:
                 arrival(a, n, targets[n]).start()
 
-    qgain, kgain = qgain_ref[pl.ds(me, 1), :], kgain_ref[pl.ds(me, 1), :]
-    dk_ref[...] = jnp.zeros_like(dk_ref)
-    dv_ref[...] = jnp.zeros_like(dv_ref)
-    gq_ref[...] = jnp.zeros_like(gq_ref)
-    part_ref[...] = jnp.zeros_like(part_ref)
+    for fetch in fetches:
+        fetch.wait()
+    qgain, kgain = qgain_ref[...], kgain_ref[...]
     spans = []
     for i in range(2):
         first = start_ref[core, i]
@@ -197,7 +215,7 @@
     for n in range(1, MEMBERS):
         arrival(4, n, targets[n]).wait_recv()
     for n in range(MEMBERS):
-        row = places[n]
+        row = places[n].astype(F32)
         limit = row + 1.0
         for start, end in spans:
             limit = jnp.where((row >= start) & (row < end), end, limit)
@@ -345,21 +363,31 @@
             back(i, n, (yy, zz), yy * 8 + zz).wait()
 
 
+def hand_over(*refs):
+    sems = refs[-1]
+    copies = [pltpu.make_async_copy(refs[i], refs[5 + i], sems.at[i]) for i in range(5)]
+    for copy in copies:
+        copy.start()
+    for copy in copies:
+        copy.wait()
+
+
 def body(query_rows, key_rows, value_rows, cotangent, query_gain, key_gain, positions, span_start, span_length):
     rows = query_rows.shape[0]
     vmem = pl.BlockSpec(memory_space=pltpu.VMEM)
-    smem = pl.BlockSpec(memory_space=pltpu.SMEM)
-    hbm = pl.BlockSpec(memory_space=pl.ANY)
+    hbm = pl.BlockSpec(memory_space=pltpu.HBM)
+    free = pl.BlockSpec(memory_space=pl.ANY)
     row_array = jax.ShapeDtypeStruct((rows, HEADS * HEAD), BF16)
     dma = pltpu.SemaphoreType.DMA
-    return pl.pallas_call(
+    results = row_array, row_array, row_array, row_array, jax.ShapeDtypeStruct((2, HEADS * HEAD), F32)
+    landed = pl.pallas_call(
         fused_kernel,
-        out_shape=(row_array,) * 4 + (jax.ShapeDtypeStruct((2, HEADS * HEAD), F32),),
-        in_specs=[smem] * 2 + [hbm] * 4 + [vmem] * 3,
-        out_specs=(hbm,) * 4 + (vmem,),
+        out_shape=results,
+        in_specs=[hbm] * 9,
+        out_specs=(free,) * 4 + (vmem,),
         scratch_shapes=[
             pltpu.VMEM((4, MEMBERS, TOK, HEAD), BF16),
-            pltpu.VMEM((MEMBERS, 1, TOK), F32),
+            pltpu.VMEM((MEMBERS, 1, TOK), jnp.int32),
             pltpu.VMEM((4, MEMBERS, TOK, HEAD), BF16),
             pltpu.VMEM((LEN, HEAD), BF16),
             pltpu.VMEM((HEAD, LEN), BF16),
@@ -375,6 +403,11 @@
             pltpu.VMEM((MEMBERS, 8, HEAD), F32),
             pltpu.VMEM((8, HEAD), F32),
             pltpu.VMEM((MEMBERS, 8, HEAD), F32),
+            pltpu.SMEM((SEQS, SPANS), jnp.int32),
+            pltpu.SMEM((SEQS, SPANS), jnp.int32),
+            pltpu.VMEM((1, HEAD), F32),
+            pltpu.VMEM((1, HEAD), F32),
+            dma((4,)),
             dma((5, MEMBERS)),
             dma((5, MEMBERS)),
             dma((4, MEMBERS)),
@@ -383,12 +416,25 @@
             dma((2, MEMBERS)),
         ],
         compiler_params=pltpu.CompilerParams(
-            collective_id=0, has_side_effects=True, vmem_limit_bytes=40 << 20
+            collective_id=0, has_side_effects=True, vmem_limit_bytes=GRANT
         ),
     )(
-        span_start, span_length, query_rows, key_rows, value_rows, cotangent,
-        positions.astype(F32).reshape(1, TOK), query_gain.reshape(HEADS, HEAD), key_gain.reshape(HEADS, HEAD),
+        *(
+            pltpu.with_memory_space_constraint(t, pltpu.HBM)
+            for t in (
+                span_start, span_length, query_rows, key_rows, value_rows, cotangent,
+                positions.reshape(1, TOK), query_gain.reshape(HEADS, HEAD), key_gain.reshape(HEADS, HEAD),
+            )
+        )
     )
+    return pl.pallas_call(
+        hand_over,
+        out_shape=results,
+        in_specs=[free] * 5,
+        out_specs=(hbm,) * 5,
+        scratch_shapes=[dma((5,))],
+        compiler_params=pltpu.CompilerParams(vmem_limit_bytes=1 << 20),
+    )(*landed)
 
 
 def solution(mesh):

time: 121 us -> 111 us (0.917)
  local copies, waits for them, and re-layouts: 10.7 us -> 0 us
  Pallas kernels: 109 us -> 111 us
    unnamed x23 -> x0, local copies, waits for them, and re-layouts: 10.7 us -> none
    pallas_call x1 -> x2, Pallas kernels: 109 us -> 111 us  [the longest x1 109 us: body(): pl.pallas_call(fused_kernel, out_shape=results, in_specs=[hbm] * 9, out_s...]
where the time goes in v3:
time: 111 us
  Pallas kernels  111 us (100%)
    pallas_call x1, Pallas kernels, body(): pl.pallas_call(fused_kernel, out_shape=results, in_specs=[hbm] * 9, out_s...  109 us

profile of v3, /device:TPU:32, one launch (start us, length us, event | category | flops | bytes accessed | tf_op | source)
XLA Modules:
  0.0 111.3 jit_solution(10513131210951898890)
XLA Ops:
  0.6 109.3 %shard_map.128 = (bf16[128,2048]{1,0:T(8,128)(2,1)S(1)}, bf16[128,2048]{1,0:T(8,128)(2,1)S(1)}, bf16[128,2048]{1,0:T(8,128)(2,1)S(1)}, bf16[128,2048]{1,0:T(8,128)(2,1)S(1)}, f32[2,2048]{1,0:T(2,128)S(1)}) custom-call(s32[2,2]{1,0:T(2,128)} %start_hbm.1, s32[2,2]{1,0:T(2,128)} %length_hbm.1, bf16[128,2048]{1,0:T(8,128)(2,1)} %q_hbm.1, ...), custom_call_target="tpu_custom_call" | custom-call | tf_op jit(solution)/shard_map/pallas_call | solution.py:383
  110.0 1.4 %shard_map.129 = (bf16[128,2048]{1,0:T(8,128)(2,1)}, bf16[128,2048]{1,0:T(8,128)(2,1)}, bf16[128,2048]{1,0:T(8,128)(2,1)}, bf16[128,2048]{1,0:T(8,128)(2,1)}, f32[2,2048]{1,0:T(2,128)}) custom-call(bf16[128,2048]{1,0:T(8,128)(2,1)S(1)} %get-tuple-element.10.refs_0_, bf16[128,2048]{1,0:T(8,128)(2,1)S(1)} %get-tuple-element.11.refs_1_, ...), custom_call_target="tpu_custom_call" | custom-call | tf_op jit(solution)/shard_map/pallas_call | solution.py:430

commit v4 on v3

--- a/solution.py
+++ b/solution.py
@@ -29,6 +29,7 @@
 KC = 256
 CHUNKS = LEN // KC
 GRANT = 40 << 20
+HELD = 8
 
 
 def unit_of(raw):
@@ -134,12 +135,12 @@
     start_hbm, length_hbm, q_hbm, k_hbm, v_hbm, do_hbm, place_ref, qgain_hbm, kgain_hbm,
     out_hbm, gq_hbm, gk_hbm, gv_hbm, gains_ref,
     recv, places, send, kn_ref, knT_ref, vT_ref, kpos_ref, limit_ref, s_ref, p_ref, dk_ref, dv_ref, gq_ref,
-    part_ref, parts, whole_ref, wholes, start_ref, length_ref, qgain_ref, kgain_ref, small, in_send, in_recv, back_send, back_recv, gain_send, gain_recv,
+    sums, others, wholes, start_ref, length_ref, qgain_ref, kgain_ref, small, in_send, in_recv, back_send, back_recv,
+    pair_send, pair_recv, gain_send, gain_recv, rounds,
 ):
     y, z, core = lax.axis_index("ctx_0"), lax.axis_index("ctx_1"), lax.axis_index("ctx_2")
     d0, d1 = lax.axis_index("dp_0"), lax.axis_index("dp_1")
     me = y * 8 + z
-    member = d0 * 8 + d1 * 2 + core
 
     def target(n):
         return lax.rem(y + lax.rem(n, 2), 2), lax.rem(z + across(lax.div(n, 2)), 8)
@@ -147,18 +148,38 @@
     def origin(n):
         return lax.rem(y + lax.rem(n, 2), 2), lax.rem(z + 8 - across(lax.div(n, 2)), 8)
 
-    def sibling(t):
-        return {
-            "dp_0": lax.rem(d0 + t // 8, 2),
-            "dp_1": lax.rem(d1 + t // 2 % 4, 4),
-            "ctx_2": lax.rem(core + t % 2, 2),
-        }
-
+    kin = (
+        {"ctx_2": 1 - core},
+        {"dp_1": d1 + 1 - 2 * lax.rem(d1, 2)},
+        {"dp_1": 3 - d1},
+        {"dp_0": 1 - d0},
+    )
     targets = [target(jnp.int32(n)) for n in range(MEMBERS)]
+    sides = [device(*targets[2]), device(*targets[4])]
     barrier = pltpu.get_barrier_semaphore()
-    for n in range(1, MEMBERS):
-        pl.semaphore_signal(barrier, inc=1, device_id=device(*targets[n]), device_id_type=MESH)
-        pl.semaphore_signal(barrier, inc=1, device_id=sibling(n), device_id_type=MESH)
+    for at in (*sides, device(*targets[1]), *kin):
+        pl.semaphore_signal(barrier, inc=1, device_id=at, device_id_type=MESH)
+
+    def incoming(a, n, at):
+        if a == 4:
+            source, dest = place_ref, places.at[n]
+        else:
+            source, dest = (q_hbm, k_hbm, v_hbm, do_hbm)[a], recv.at[a, n]
+            source = source.at[:, columns(at[0] * 8 + at[1])]
+        return source, dest
+
+    def arrival(a, n, at):
+        source, dest = incoming(a, n, at)
+        return pltpu.make_async_remote_copy(
+            source, dest, in_send.at[a, n], in_recv.at[a, n], device_id=device(*at), device_id_type=MESH
+        )
+
+    def own(a):
+        source, dest = incoming(a, 0, (y, z))
+        return pltpu.make_async_copy(source, dest, in_recv.at[a, 0])
+
+    for a in (4, 1, 2, 0, 3):
+        own(a).start()
     fetches = [
         pltpu.make_async_copy(source, dest, small.at[i])
         for i, (source, dest) in enumerate(
@@ -172,37 +193,24 @@
     ]
     for fetch in fetches:
         fetch.start()
+    pl.semaphore_wait(barrier, 3 + len(kin))
+
+    for r, known in enumerate(((1, 2, 4), (3, 5, 6, 8), (7, 9, 10, 12), (11, 13, 14), (15,))):
+        if r > 0:
+            pl.semaphore_wait(rounds.at[r - 1], 2)
+        if r < 4:
+            for at in sides:
+                pl.semaphore_signal(rounds.at[r], inc=1, device_id=at, device_id_type=MESH)
+        for n in known:
+            for a in (4, 1, 2):
+                arrival(a, n, targets[n]).start()
+    for n in range(1, MEMBERS):
+        for a in (0, 3):
+            arrival(a, n, targets[n]).start()
+
     dk_ref[...] = jnp.zeros_like(dk_ref)
     dv_ref[...] = jnp.zeros_like(dv_ref)
     gq_ref[...] = jnp.zeros_like(gq_ref)
-    part_ref[...] = jnp.zeros_like(part_ref)
-    pl.semaphore_wait(barrier, 2 * (MEMBERS - 1))
-
-    def incoming(a, n, at):
-        if a == 4:
-            source, dest = place_ref, places.at[n]
-        else:
-            source, dest = (q_hbm, k_hbm, v_hbm, do_hbm)[a], recv.at[a, n]
-            source = source.at[:, columns(at[0] * 8 + at[1])]
-        return source, dest
-
-    def arrival(a, n, at):
-        source, dest = incoming(a, n, at)
-        return pltpu.make_async_remote_copy(
-            source, dest, in_send.at[a, n], in_recv.at[a, n], device_id=device(*at), device_id_type=MESH
-        )
-
-    def own(a):
-        source, dest = incoming(a, 0, (y, z))
-        return pltpu.make_async_copy(source, dest, in_recv.at[a, 0])
-
-    for group in ((4,), (1,), (2,), (0, 3)):
-        for a in group:
-            own(a).start()
-        for n in range(1, MEMBERS):
-            for a in group:
-                arrival(a, n, targets[n]).start()
-
     for fetch in fetches:
         fetch.wait()
     qgain, kgain = qgain_ref[...], kgain_ref[...]
@@ -292,69 +300,62 @@
         def _():
             send_step(b - 1)
 
-    for n in range(MEMBERS):
-        send[3, n] = dv_ref[n * TOK : (n + 1) * TOK, :].astype(BF16)
+    def results(i, n):
+        if n == 0:
+            stays(i).start()
+        else:
+            back(i, n, origin(jnp.int32(n)), me).start()
+
+    def exchange(e):
+        return pltpu.make_async_remote_copy(
+            sums.at[e], others.at[e], pair_send.at[e], pair_recv.at[e], device_id=kin[e], device_id_type=MESH
+        )
+
+    def publish(n):
+        return pltpu.make_async_remote_copy(
+            sums.at[len(kin)], wholes.at[me], gain_send.at[n], gain_recv.at[n],
+            device_id=device(*targets[n]), device_id_type=MESH,
+        )
+
     send_step(jnp.int32(STEPS - 1))
     gk = jnp.zeros((1, HEAD), F32)
     for n in range(MEMBERS):
         grad, part = norm_back(dk_ref[n * TOK : (n + 1) * TOK, :] * SCALE, recv[1, n], kgain)
         gk = gk + part
         send[2, n] = grad
-        if n == 0:
-            part_ref[0:1, :] = gq_ref[...]
-            stays(3).start()
-        else:
-            back(3, n, origin(jnp.int32(n)), me).start()
-    part_ref[1:2, :] = gk
-    parts[member] = part_ref[...]
-
-    def half(n):
-        if n == 0:
-            stays(2).start()
-        else:
-            back(2, n, origin(jnp.int32(n)), me).start()
-
-    def spread(t):
-        return pltpu.make_async_remote_copy(
-            part_ref, parts.at[member], gain_send.at[0, t], gain_recv.at[0, t],
-            device_id=sibling(t), device_id_type=MESH,
-        )
-
-    def publish(n):
-        return pltpu.make_async_remote_copy(
-            whole_ref, wholes.at[me], gain_send.at[1, n], gain_recv.at[1, n],
-            device_id=device(*targets[n]), device_id_type=MESH,
-        )
-
-    for n in range(4):
-        half(n)
-    for t in range(1, MEMBERS):
-        spread(t).start()
-    for n in range(4, 8):
-        half(n)
-    for t in range(1, MEMBERS):
-        spread(t).wait_recv()
-    whole = parts[0]
-    for t in range(1, MEMBERS):
-        whole = whole + parts[t]
-    whole_ref[...] = whole
-    wholes[me] = whole
-    for n in range(8, 12):
-        half(n)
+    sums[0] = jnp.concatenate([gq_ref[...], gk, jnp.zeros((6, HEAD), F32)], axis=0)
+    for n in range(MEMBERS):
+        send[3, n] = dv_ref[n * TOK : (n + 1) * TOK, :].astype(BF16)
+    for e in range(len(kin)):
+        exchange(e).start()
+        if e == len(kin) - 1:
+            for n in range(3 * e, MEMBERS):
+                results(3, n)
+            for n in range(MEMBERS - HELD):
+                results(2, n)
+        exchange(e).wait_recv()
+        sums[e + 1] = sums[e] + others[e]
+        if e < len(kin) - 1:
+            for n in range(3 * e, 3 * e + 3):
+                results(3, n)
+    wholes[me] = sums[len(kin)]
+    for n in range(MEMBERS - HELD, MEMBERS - HELD + 2):
+        results(2, n)
     for n in range(1, MEMBERS):
         publish(n).start()
-    for n in range(12, MEMBERS):
-        half(n)
+    for n in range(MEMBERS - HELD + 2, MEMBERS):
+        results(2, n)
     for n in range(1, MEMBERS):
         publish(n).wait_recv()
     for h in range(HEADS):
         gains_ref[:, h * HEAD : (h + 1) * HEAD] = wholes[h, 0:2, :]
 
     for n in range(1, MEMBERS):
-        spread(n).wait_send()
         publish(n).wait_send()
         for a in range(5):
             arrival(a, n, targets[n]).wait_send()
+    for e in range(len(kin)):
+        exchange(e).wait_send()
     for i in range(4):
         stays(i).wait()
     for n in range(1, MEMBERS):
@@ -399,9 +400,8 @@
             pltpu.VMEM((LEN, HEAD), F32),
             pltpu.VMEM((LEN, HEAD), F32),
             pltpu.VMEM((1, HEAD), F32),
-            pltpu.VMEM((8, HEAD), F32),
-            pltpu.VMEM((MEMBERS, 8, HEAD), F32),
-            pltpu.VMEM((8, HEAD), F32),
+            pltpu.VMEM((5, 8, HEAD), F32),
+            pltpu.VMEM((4, 8, HEAD), F32),
             pltpu.VMEM((MEMBERS, 8, HEAD), F32),
             pltpu.SMEM((SEQS, SPANS), jnp.int32),
             pltpu.SMEM((SEQS, SPANS), jnp.int32),
@@ -412,8 +412,11 @@
             dma((5, MEMBERS)),
             dma((4, MEMBERS)),
             dma((4, MEMBERS)),
-            dma((2, MEMBERS)),
-            dma((2, MEMBERS)),
+            dma((4,)),
+            dma((4,)),
+            dma((MEMBERS,)),
+            dma((MEMBERS,)),
+            pltpu.SemaphoreType.REGULAR((4,)),
         ],
         compiler_params=pltpu.CompilerParams(
             collective_id=0, has_side_effects=True, vmem_limit_bytes=GRANT

time: 111 us -> 109 us (0.982)
  Pallas kernels: 111 us -> 108 us
    pallas_call x1, Pallas kernels: 109 us -> 107 us  [body(): pl.pallas_call(fused_kernel, out_shape=results, in_specs=[hbm] * 9, out_s...]
where the time goes in v4:
time: 109 us
  Pallas kernels  108 us (99%)
    pallas_call x1, Pallas kernels, body(): pl.pallas_call(fused_kernel, out_shape=results, in_specs=[hbm] * 9, out_s...  107 us

profile of v4, /device:TPU:32, one launch (start us, length us, event | category | flops | bytes accessed | tf_op | source)
XLA Modules:
  0.0 108.8 jit_solution(8368926840583122872)
XLA Ops:
  0.6 106.8 %shard_map.128 = (bf16[128,2048]{1,0:T(8,128)(2,1)S(1)}, bf16[128,2048]{1,0:T(8,128)(2,1)S(1)}, bf16[128,2048]{1,0:T(8,128)(2,1)S(1)}, bf16[128,2048]{1,0:T(8,128)(2,1)S(1)}, f32[2,2048]{1,0:T(2,128)S(1)}) custom-call(s32[2,2]{1,0:T(2,128)} %start_hbm.1, s32[2,2]{1,0:T(2,128)} %length_hbm.1, bf16[128,2048]{1,0:T(8,128)(2,1)} %q_hbm.1, ...), custom_call_target="tpu_custom_call" | custom-call | tf_op jit(solution)/shard_map/pallas_call | solution.py:384
  107.4 1.4 %shard_map.129 = (bf16[128,2048]{1,0:T(8,128)(2,1)}, bf16[128,2048]{1,0:T(8,128)(2,1)}, bf16[128,2048]{1,0:T(8,128)(2,1)}, bf16[128,2048]{1,0:T(8,128)(2,1)}, f32[2,2048]{1,0:T(2,128)}) custom-call(bf16[128,2048]{1,0:T(8,128)(2,1)S(1)} %get-tuple-element.10.refs_0_, bf16[128,2048]{1,0:T(8,128)(2,1)S(1)} %get-tuple-element.11.refs_1_, ...), custom_call_target="tpu_custom_call" | custom-call | tf_op jit(solution)/shard_map/pallas_call | solution.py:433

commit v5 on v4

--- a/solution.py
+++ b/solution.py
@@ -86,31 +86,31 @@
         top = jnp.maximum(top, fold8(s, jnp.max))
     top = jnp.max(top, axis=0, keepdims=True)
     total = jnp.zeros((8, QB), F32)
+    for j in range(CHUNKS):
+        rows = slice(j * KC, (j + 1) * KC)
+        total = total + fold8(jnp.exp2(s_ref[rows, :] - top), jnp.sum)
+    top = top + jnp.log2(jnp.sum(total, axis=0, keepdims=True))
     oT = jnp.zeros((HEAD, QB), F32)
     for j in range(CHUNKS):
         rows = slice(j * KC, (j + 1) * KC)
         p = jnp.exp2(s_ref[rows, :] - top)
-        total = total + fold8(p, jnp.sum)
-        pb = p.astype(BF16)
-        p_ref[rows, :] = pb
-        oT = oT + dot(vT_ref[:, rows], pb)
-    inv = 1.0 / jnp.sum(total, axis=0, keepdims=True)
-    oT = (oT * inv).astype(BF16).astype(F32)
+        s_ref[rows, :] = p
+        weights = p.astype(BF16)
+        p_ref[rows, :] = weights
+        oT = oT + dot(vT_ref[:, rows], weights)
+    oT = oT.astype(BF16).astype(F32)
     out = oT.T.astype(BF16)
-    gradT = do_ref[pl.ds(b * PER, PER)].reshape(QB, HEAD).astype(F32).T * inv
-    gT = gradT.astype(BF16)
-    gT32 = gT.astype(F32)
-    g = gT32.T.astype(BF16)
+    g = do_ref[pl.ds(b * PER, PER)].reshape(QB, HEAD)
+    gT32 = g.astype(F32).T
+    gT = gT32.astype(BF16)
     delta = jnp.sum(oT * gT32, axis=0, keepdims=True)
     dqT = jnp.zeros((HEAD, QB), F32)
     for j in range(CHUNKS):
         rows = slice(j * KC, (j + 1) * KC)
         per = KC // TOK
         vj = v_ref[j * per : (j + 1) * per].reshape(KC, HEAD)
-        dp = dot(vj, gT)
-        pb = p_ref[rows, :]
-        ds = (pb.astype(F32) * (dp - delta)).astype(BF16)
-        dv_ref[rows, :] += dot(pb, g)
+        ds = (s_ref[rows, :] * (dot(vj, gT) - delta)).astype(BF16)
+        dv_ref[rows, :] += dot(p_ref[rows, :], g)
         dk_ref[rows, :] += dot(ds, qn)
         dqT = dqT + dot(knT_ref[:, rows], ds)
     dq = dqT.T * SCALE
@@ -317,12 +317,12 @@
             device_id=device(*targets[n]), device_id_type=MESH,
         )
 
-    send_step(jnp.int32(STEPS - 1))
     gk = jnp.zeros((1, HEAD), F32)
     for n in range(MEMBERS):
         grad, part = norm_back(dk_ref[n * TOK : (n + 1) * TOK, :] * SCALE, recv[1, n], kgain)
         gk = gk + part
         send[2, n] = grad
+    send_step(jnp.int32(STEPS - 1))
     sums[0] = jnp.concatenate([gq_ref[...], gk, jnp.zeros((6, HEAD), F32)], axis=0)
     for n in range(MEMBERS):
         send[3, n] = dv_ref[n * TOK : (n + 1) * TOK, :].astype(BF16)

time: 109 us -> 110 us (level)
  no operation moved by 1% of the time
where the time goes in v5:
time: 110 us; the launch traced here: 109 us
  Pallas kernels  109 us (99%)
    pallas_call x1, Pallas kernels, body(): pl.pallas_call(fused_kernel, out_shape=results, in_specs=[hbm] * 9, out_s...  107 us

profile of v5, /device:TPU:32, one launch (start us, length us, event | category | flops | bytes accessed | tf_op | source)
XLA Modules:
  0.0 109.2 jit_solution(13189922820489651487)
XLA Ops:
  0.6 107.2 %shard_map.128 = (bf16[128,2048]{1,0:T(8,128)(2,1)S(1)}, bf16[128,2048]{1,0:T(8,128)(2,1)S(1)}, bf16[128,2048]{1,0:T(8,128)(2,1)S(1)}, bf16[128,2048]{1,0:T(8,128)(2,1)S(1)}, f32[2,2048]{1,0:T(2,128)S(1)}) custom-call(s32[2,2]{1,0:T(2,128)} %start_hbm.1, s32[2,2]{1,0:T(2,128)} %length_hbm.1, bf16[128,2048]{1,0:T(8,128)(2,1)} %q_hbm.1, ...), custom_call_target="tpu_custom_call" | custom-call | tf_op jit(solution)/shard_map/pallas_call | solution.py:384
  107.9 1.4 %shard_map.129 = (bf16[128,2048]{1,0:T(8,128)(2,1)}, bf16[128,2048]{1,0:T(8,128)(2,1)}, bf16[128,2048]{1,0:T(8,128)(2,1)}, bf16[128,2048]{1,0:T(8,128)(2,1)}, f32[2,2048]{1,0:T(2,128)}) custom-call(bf16[128,2048]{1,0:T(8,128)(2,1)S(1)} %get-tuple-element.10.refs_0_, bf16[128,2048]{1,0:T(8,128)(2,1)S(1)} %get-tuple-element.11.refs_1_, ...), custom_call_target="tpu_custom_call" | custom-call | tf_op jit(solution)/shard_map/pallas_call | solution.py:433

commit v6 on v5

--- a/solution.py
+++ b/solution.py
@@ -323,7 +323,7 @@
         gk = gk + part
         send[2, n] = grad
     send_step(jnp.int32(STEPS - 1))
-    sums[0] = jnp.concatenate([gq_ref[...], gk, jnp.zeros((6, HEAD), F32)], axis=0)
+    sums[0] = jnp.concatenate([gq_ref[...], gk], axis=0)
     for n in range(MEMBERS):
         send[3, n] = dv_ref[n * TOK : (n + 1) * TOK, :].astype(BF16)
     for e in range(len(kin)):
@@ -348,7 +348,7 @@
     for n in range(1, MEMBERS):
         publish(n).wait_recv()
     for h in range(HEADS):
-        gains_ref[:, h * HEAD : (h + 1) * HEAD] = wholes[h, 0:2, :]
+        gains_ref[:, h * HEAD : (h + 1) * HEAD] = wholes[h]
 
     for n in range(1, MEMBERS):
         publish(n).wait_send()
@@ -400,9 +400,9 @@
             pltpu.VMEM((LEN, HEAD), F32),
             pltpu.VMEM((LEN, HEAD), F32),
             pltpu.VMEM((1, HEAD), F32),
-            pltpu.VMEM((5, 8, HEAD), F32),
-            pltpu.VMEM((4, 8, HEAD), F32),
-            pltpu.VMEM((MEMBERS, 8, HEAD), F32),
+            pltpu.VMEM((5, 2, HEAD), F32),
+            pltpu.VMEM((4, 2, HEAD), F32),
+            pltpu.VMEM((MEMBERS, 2, HEAD), F32),
             pltpu.SMEM((SEQS, SPANS), jnp.int32),
             pltpu.SMEM((SEQS, SPANS), jnp.int32),
             pltpu.VMEM((1, HEAD), F32),

time: 110 us -> 109 us (level)
  no operation moved by 1% of the time
where the time goes in v6:
time: 109 us; the launch traced here: 108 us
  Pallas kernels  108 us (99%)
    pallas_call x1, Pallas kernels, body(): pl.pallas_call(fused_kernel, out_shape=results, in_specs=[hbm] * 9, out_s...  106 us

profile of v6, /device:TPU:32, one launch (start us, length us, event | category | flops | bytes accessed | tf_op | source)
XLA Modules:
  0.0 108.2 jit_solution(413116311112741669)
XLA Ops:
  0.6 106.2 %shard_map.128 = (bf16[128,2048]{1,0:T(8,128)(2,1)S(1)}, bf16[128,2048]{1,0:T(8,128)(2,1)S(1)}, bf16[128,2048]{1,0:T(8,128)(2,1)S(1)}, bf16[128,2048]{1,0:T(8,128)(2,1)S(1)}, f32[2,2048]{1,0:T(2,128)S(1)}) custom-call(s32[2,2]{1,0:T(2,128)} %start_hbm.1, s32[2,2]{1,0:T(2,128)} %length_hbm.1, bf16[128,2048]{1,0:T(8,128)(2,1)} %q_hbm.1, ...), custom_call_target="tpu_custom_call" | custom-call | tf_op jit(solution)/shard_map/pallas_call | solution.py:384
  106.8 1.4 %shard_map.129 = (bf16[128,2048]{1,0:T(8,128)(2,1)}, bf16[128,2048]{1,0:T(8,128)(2,1)}, bf16[128,2048]{1,0:T(8,128)(2,1)}, bf16[128,2048]{1,0:T(8,128)(2,1)}, f32[2,2048]{1,0:T(2,128)}) custom-call(bf16[128,2048]{1,0:T(8,128)(2,1)S(1)} %get-tuple-element.10.refs_0_, bf16[128,2048]{1,0:T(8,128)(2,1)S(1)} %get-tuple-element.11.refs_1_, ...), custom_call_target="tpu_custom_call" | custom-call | tf_op jit(solution)/shard_map/pallas_call | solution.py:433
